TPU v7x, 512 devices: a whole 4x4x16 slice. The times are simulated.
512 devices in a mesh: gx: 8 (over y, core), gy: 16 (over z), gz: 4 (over x).
Axes of the slice: x: 4, y: 4, z: 16, core: 2. Of those that a mesh axis runs over, the one named last changes fastest.
Arguments:
- source_term: float32 [32, 32, 128, 512], P(None, 'gx', 'gy', 'gz'), may hold values from -16 to 16
- labels: int32 [32, 128, 512], P('gx', 'gy', 'gz'), may hold values from 0 to 5
- conductivity_table: float32 [6], replicated, may hold values from 0.05 to 1
- send_map: int32 [8, 16, 4, 256], P('gx', 'gy', 'gz'), may hold values from -1 to 4095, as said below
- owner_slots: int32 [65536], P(('gx', 'gy', 'gz')), may hold values from 0 to 255, as said below
- sensor_data: float32 [32, 128], replicated, may hold values from -6 to 6
Outputs:
- projections: float32 [3, 128, 65536], P(None, None, ('gx', 'gy', 'gz'))
- gram_blocks: float32 [6, 65536], P(None, ('gx', 'gy', 'gz'))
Inputs may be any that keep to these rules, and one draw needn't show every extreme that they name: `send_map`: entries q * 2 to q * 2 + 1 of row (sx, sy, iz) hold, in their first slots, the brick-local voxels (i * 8 + j) * 128 + k of the positions that this brick sends to owner q = ix * 16 + iy of the same iz, and -1 in the others; no voxel appears twice in a row; some brick fills all 2 slots of some owner. `owner_slots`: the 128 entries of owner d = (ix * 16 + iy) * 4 + iz name, each once, exactly the slots src * 2 + slot that the bricks src = sx * 16 + sy with the same iz fill for it.
All inputs are finite; a program needn't handle non-finite values.
Results may differ from a plain program's by a relative error of at most 0.00012.
Values sent between devices are 32-bit elements; how exact they have to be, the bound alone decides.
A program may use at most 64 MiB of HBM per device.

v0:
```python
import jax
import jax.numpy as jnp
from jax import lax
from jax.sharding import Mesh
from jax.sharding import PartitionSpec as P

GX_GY_GZ = ("gx_0", "gx_1", "gy", "gz")
GX = ("gx_0", "gx_1")
GX_GY = ("gx_0", "gx_1", "gy")


mass_term = 0.25


def extended(block, sides, width):
    for axis, dim in sides:
        count = lax.axis_size(axis)
        forward = [(i, i + 1) for i in range(count - 1)]
        backward = [(target, source) for source, target in forward]
        low = lax.ppermute(
            lax.slice_in_dim(block, block.shape[dim] - width, None, axis=dim), axis, forward
        )
        high = lax.ppermute(lax.slice_in_dim(block, 0, width, axis=dim), axis, backward)
        block = jnp.concatenate([low, block, high], axis=dim)
    return block


def by_axis(x, axes):
    for axis in axes:
        x = lax.psum(x, axis)
    return x


def tissue(shifted, table):
    conductivity = jnp.zeros(shifted.shape, table.dtype)
    for tissue_level in range(table.shape[0]):
        conductivity = conductivity + jnp.where(
            shifted == tissue_level + 1, table[tissue_level], 0.0
        )
    inside = (shifted > 0).astype(table.dtype)
    return (conductivity, inside)


def neighbour_slices(dim_index, offset):
    selection = [slice(1, -1), slice(1, -1), slice(1, -1)]
    selection[dim_index] = slice(2, None) if offset > 0 else slice(0, -2)
    return tuple(selection)


def stencil(padded, conductivity, inside):
    leading = (slice(None),) * (padded.ndim - 3)
    middle = (slice(1, -1), slice(1, -1), slice(1, -1))
    centre = padded[leading + middle]
    own_cond = conductivity[middle]
    own_in = inside[middle]
    accumulated = mass_term * centre
    for dim_index in range(3):
        for offset in (-1, 1):
            beside_all = neighbour_slices(dim_index, offset)
            weight = 0.5 * (own_cond + conductivity[beside_all]) * own_in * inside[beside_all]
            accumulated = accumulated + weight * (centre - padded[leading + beside_all])
    return accumulated


def gram_rows(leadfield):
    entry_pairs = ((0, 0), (1, 1), (2, 2), (0, 1), (0, 2), (1, 2))
    return jnp.stack(
        [jnp.sum(leadfield[first] * leadfield[second], axis=0) for first, second in entry_pairs]
    )


def local_inner(first, second):
    return jnp.sum(first * second, axis=(1, 2, 3))


def per_sensor(values):
    return values[:, None, None, None]


def per_device(source_term, labels, conductivity_table, send_map, owner_slots, sensor_data):
    sensors, size_x, size_y, size_z = source_term.shape
    shifted = labels + 1
    label_pad = extended(shifted, ((GX, 0), ("gy", 1), ("gz", 2)), 2)
    conductivity, inside = tissue(label_pad, conductivity_table)
    source_pad = extended(source_term, ((GX, 1), ("gy", 2), ("gz", 3)), 2)
    applied = stencil(source_pad, conductivity, inside)
    inner_cond = conductivity[1:-1, 1:-1, 1:-1]
    inner_in = inside[1:-1, 1:-1, 1:-1]
    twice_applied = stencil(applied, inner_cond, inner_in)
    applied_core = applied[:, 1:-1, 1:-1, 1:-1]
    moment_zero, moment_one, moment_two, moment_three = (
        by_axis(local_inner(source_term, source_term), GX_GY_GZ),
        by_axis(local_inner(source_term, applied_core), GX_GY_GZ),
        by_axis(local_inner(applied_core, applied_core), GX_GY_GZ),
        by_axis(local_inner(applied_core, twice_applied), GX_GY_GZ),
    )
    first_step = moment_zero / moment_one
    residue = first_step * first_step * moment_two - moment_zero
    growth = 1.0 + residue / moment_zero
    curvature = (
        growth * growth * moment_one
        - 2.0 * growth * first_step * moment_two
        + first_step * first_step * moment_three
    )
    second_step = residue / curvature
    source_coef = first_step + second_step * growth
    applied_coef = second_step * first_step
    solution_pad = (
        per_sensor(source_coef) * source_pad[:, 1:-1, 1:-1, 1:-1]
        - per_sensor(applied_coef) * applied
    )
    cond_inner = conductivity[2:-2, 2:-2, 2:-2]
    voxel_local = jnp.maximum(send_map.reshape(-1), 0)
    index_x = voxel_local // (size_y * size_z)
    index_y = voxel_local // size_z % size_y
    index_z = voxel_local % size_z
    stride_y = size_z + 2
    stride_x = (size_y + 2) * (size_z + 2)
    centre = (index_x + 1) * stride_x + (index_y + 1) * stride_y + (index_z + 1)
    flattened = solution_pad.reshape(sensors, -1)
    cond_here = jnp.take(cond_inner.reshape(-1), voxel_local)

    def gradient(stride):
        upper = jnp.take(flattened, centre + stride, axis=1)
        lower = jnp.take(flattened, centre - stride, axis=1)
        return cond_here * ((upper - lower) * 0.5)

    columns = jnp.stack([gradient(stride_x), gradient(stride_y), gradient(1)])
    received = lax.all_to_all(columns, GX_GY, split_axis=2, concat_axis=2, tiled=True)
    owned = jnp.take(received, owner_slots, axis=2)
    projections = jnp.einsum("csp,st->ctp", owned, sensor_data, precision=lax.Precision.HIGHEST)
    return (projections, gram_rows(owned))


def solution(mesh):
    split = Mesh(
        mesh.devices.reshape(4, 2, mesh.shape["gy"], mesh.shape["gz"]), ("gx_0", "gx_1", "gy", "gz")
    )
    in_specs = (
        P(None, GX, "gy", "gz"),
        P(GX, "gy", "gz"),
        P(),
        P(GX, "gy", "gz", None),
        P(GX_GY_GZ),
        P(),
    )
    out_specs = (P(None, None, GX_GY_GZ), P(None, GX_GY_GZ))
    return jax.shard_map(
        per_device, mesh=split, in_specs=in_specs, out_specs=out_specs, check_vma=False
    )
```

profile of v0, /device:TPU:1, one launch (start us, length us, event | category | flops | bytes accessed | tf_op | source)
XLA Modules:
  0.0 224.1 jit_solution(13874952597590977932)
XLA Ops:
  0.6 0.7 broadcast_add_fusion
  1.4 4.6 %collective-permute-start.6 = (s32[2,8,128]{2,1,0:T(8,128)S(1)}, s32[2,8,128]{2,1,0:T(8,128)S(1)}, u32[]{:S(2)}, u32[]{:S(2)}) collective-permute-start(s32[2,8,128]{2,1,0:T(8,128)S(1)} %get-tuple-element.70), channel_id=1, source_target_pairs={{0,64},{64,128},{128,192},{192,256},{256,320},{320,384},{384,448},... | collective-permute-start | bytes 24584 | tf_op jit(solution)/shard_map/ppermute | solution.py:20
  6.0 5.5 %collective-permute-start.7 = (s32[2,8,128]{2,1,0:T(8,128)S(1)}, s32[2,8,128]{2,1,0:T(8,128)S(1)}, u32[]{:S(2)}, u32[]{:S(2)}) collective-permute-start(s32[2,8,128]{2,1,0:T(8,128)S(1)} %get-tuple-element.71), channel_id=1, source_target_pairs={{64,0},{128,64},{192,128},{256,192},{320,256},{384,320},{448,384},... | collective-permute-start | bytes 24584 | tf_op jit(solution)/shard_map/ppermute | solution.py:23
  11.4 1.1 fusion.70
  12.5 1.9 collective-permute-start
  14.4 2.4 %collective-permute-start.1 = (f32[32,2,8,128]{3,2,1,0:T(8,128)S(1)}, f32[32,2,8,128]{3,2,1,0:T(8,128)S(1)}, u32[]{:S(2)}, u32[]{:S(2)}) collective-permute-start(f32[32,2,8,128]{3,2,1,0:T(8,128)S(1)} %get-tuple-element.52), channel_id=1, source_target_pairs={{64,0},{128,64},{192,128},{256,192},{320,256},{384,320},{448,384},... | collective-permute-start | bytes 786440 | tf_op jit(solution)/shard_map/ppermute | solution.py:23
  16.9 1.9 multiply_reduce_fusion.2
  18.8 0.7 compare_reduce_fusion
  19.5 0.7 broadcast_maximum_fusion
  21.3 1.5 fusion.73
  24.0 1.3 collective-permute-start.8
  25.3 1.3 collective-permute-start.9
  27.2 2.6 %collective-permute-done.9 = s32[8,2,128]{2,1,0:T(2,128)S(1)} collective-permute-done((s32[8,2,128]{2,1,0:T(2,128)S(1)}, s32[8,2,128]{2,1,0:T(2,128)S(1)}, u32[]{:S(2)}, u32[]{:S(2)}) %collective-permute-start.9) | collective-permute-done | bytes 8224 | tf_op jit(solution)/shard_map/ppermute | solution.py:23
  30.0 3.1 %collective-permute-start.10 = (s32[8,12,2]{2,1,0:T(8,128)S(1)}, s32[8,12,2]{2,1,0:T(8,128)S(1)}, u32[]{:S(2)}, u32[]{:S(2)}) collective-permute-start(s32[8,12,2]{2,1,0:T(8,128)S(1)} %get-tuple-element.66), channel_id=1, source_target_pairs={{0,1},{1,2},{2,3},{4,5},{5,6},{6,7},{8,9},{9,10},{10,11},{12,13},{... | collective-permute-start | bytes 2312 | tf_op jit(solution)/shard_map/ppermute | solution.py:20
  33.1 1.3 collective-permute-start.11
  34.4 1.2 copy.105
  35.6 3.3 %collective-permute-done.11 = s32[8,12,2]{2,1,0:T(8,128)S(1)} collective-permute-done((s32[8,12,2]{2,1,0:T(8,128)S(1)}, s32[8,12,2]{2,1,0:T(8,128)S(1)}, u32[]{:S(2)}, u32[]{:S(2)}) %collective-permute-start.11) | collective-permute-done | bytes 800 | tf_op jit(solution)/shard_map/ppermute | solution.py:23
  39.1 3.9 %select_add_fusion = f32[8,12,132]{2,1,0:T(8,128)S(1)} fusion(f32[]{:T(128)} %bitcast.8, f32[]{:T(128)} %bitcast.7, f32[]{:T(128)} %bitcast.6, f32[]{:T(128)} %bitcast.5, f32[]{:T(128)} %bitcast.4, f32[]{:T(128)} %bitcast.3, s32[8,12,2]{2,1,0:T(8,128)S(1)} %collective-permute-done.11, s32[8,2,128]{2,1,0:T(2,128)S(1)} %collective-permute-done.9, ...), kind=kLoop, calls=%fused_computation.79 | loop fusion | flops 291456 | bytes 101400 | tf_op jit(solution)/shard_map/add | solution.py:37
  43.0 0.7 slice_multiply_fusion.11
  44.5 3.6 %collective-permute-start.2 = (f32[32,8,2,128]{3,1,2,0:T(8,128)S(1)}, f32[32,8,2,128]{3,1,2,0:T(8,128)S(1)}, u32[]{:S(2)}, u32[]{:S(2)}) collective-permute-start(f32[32,8,2,128]{3,1,2,0:T(8,128)S(1)} %get-tuple-element.49), channel_id=1, source_target_pairs={{0,4},{4,8},{8,12},{12,16},{16,20},{20,24},{24,28},{28,32},{32,36}... | collective-permute-start | bytes 786440 | tf_op jit(solution)/shard_map/ppermute | solution.py:20
  48.0 1.3 collective-permute-start.3
  49.3 0.7 slice_multiply_fusion.7
  50.0 1.7 gather_fusion
  52.0 1.1 collective-permute-done.2
  53.1 5.7 %collective-permute-done.3 = f32[32,8,2,128]{3,1,2,0:T(8,128)S(1)} collective-permute-done((f32[32,8,2,128]{3,1,2,0:T(8,128)S(1)}, f32[32,8,2,128]{3,1,2,0:T(8,128)S(1)}, u32[]{:S(2)}, u32[]{:S(2)}) %collective-permute-start.3) | collective-permute-done | bytes 262176 | tf_op jit(solution)/shard_map/ppermute | solution.py:23
  58.8 0.7 copy-done.11
  59.9 1.7 fusion.69
  61.6 2.2 copy.93
  63.9 0.9 copy.94
  64.7 1.3 collective-permute-start.5
  66.0 4.2 %collective-permute-start.4 = (f32[32,8,12,2]{0,1,3,2:T(8,128)S(1)}, f32[32,8,12,2]{0,1,3,2:T(8,128)S(1)}, u32[]{:S(2)}, u32[]{:S(2)}) collective-permute-start(f32[32,8,12,2]{0,1,3,2:T(8,128)S(1)} %copy.93), channel_id=1, source_target_pairs={{0,1},{1,2},{2,3},{4,5},{5,6},{6,7},{8,9},{9,10},{10,11},{12,13},{... | collective-permute-start | bytes 73736 | tf_op jit(solution)/shard_map/ppermute | solution.py:20
  72.6 0.6 copy.107
  73.2 0.7 copy.98
  73.8 0.7 copy.99
  74.5 0.7 copy.97
  75.2 0.7 copy.101
  75.9 0.7 copy.100
  76.6 2.4 %copy.95 = f32[32,8,12,2]{3,1,2,0:T(8,128)} copy(f32[32,8,12,2]{0,1,3,2:T(8,128)S(1)} %collective-permute-done.4) | data formatting | bytes 49152 | tf_op jit(solution)/shard_map/ppermute | solution.py:20
  78.9 2.4 %copy.96 = f32[32,8,12,2]{3,1,2,0:T(8,128)} copy(f32[32,8,12,2]{0,1,3,2:T(8,128)S(1)} %collective-permute-done.5) | data formatting | bytes 49152 | tf_op jit(solution)/shard_map/ppermute | solution.py:23
  81.4 4.8 %pad_maximum_fusion = f32[32,8,12,132]{3,1,2,0:T(8,128)S(1)} fusion(f32[32,8,12,2]{3,1,2,0:T(8,128)} %copy.96, f32[32,8,2,128]{3,1,2,0:T(8,128)} %copy-done.11, f32[32,2,8,128]{3,1,2,0:T(2,128)} %copy-done.7, f32[32,4,8,128]{3,1,2,0:T(4,128)} %copy-done.4, f32[32,2,8,128]{3,1,2,0:T(2,128)S(1)} %copy.90, f32[32,8,2,128]{3,1,2,0:T(8,128)} %copy-done.9, ...), kind=kLoop, calls=%fused_computation.8 | loop fusion | flops 2433024 | bytes 3244032 | tf_op jit(solution)/shard_map/concatenate | solution.py:24
  86.3 7.2 %fusion.2 = f32[32,6,10,130]{3,1,2,0:T(8,128)S(1)} fusion(f32[32,8,12,2]{3,1,2,0:T(8,128)S(1)} %copy-done.3, f32[32,8,2,128]{3,1,2,0:T(8,128)S(1)} %copy-done.12, f32[32,8,2,128]{3,1,2,0:T(8,128)S(1)} %copy-done.10, f32[32,2,8,128]{3,1,2,0:T(2,128)S(1)} %copy-done.8, f32[32,4,8,128]{3,1,2,0:T(4,128)S(1)} %copy-done.5, f32[32,2,8,128]{3,1,2,0:T(2,128)S(1)} %copy.90, ...), kind=kLoop, calls=%fused_computation.12 | loop fusion | flops 7238400 | bytes 7799616 | tf_op jit(solution)/shard_map/add | solution.py:61
  93.6 1.5 copy-done.1
  95.1 2.4 %multiply_reduce_fusion.1 = (f32[32]{0:T(128)S(1)}, f32[32]{0:T(128)S(1)}, f32[32]{0:T(128)S(1)}) fusion(f32[32,6,10,130]{3,1,2,0:T(8,128)S(1)} %fusion.2, f32[32,4,8,128]{3,2,1,0:T(8,128)S(1)} %copy-done.6, f32[4,8,128]{2,0,1:T(4,128)S(1)} %copy.111, f32[4,8,128]{2,0,1:T(4,128)S(1)} %copy.110, f32[4,8,128]{2,0,1:T(4,128)S(1)} %copy-done.19, ...), kind=kLoop, calls=%fused_computation.60 | loop fusion | flops 3276704 | bytes 4292992 | tf_op jit(solution)/shard_map/reduce_sum | solution.py:73
  97.5 6.0 %all-reduce.2 = (f32[32]{0:T(128)S(1)}, f32[32]{0:T(128)S(1)}, f32[32]{0:T(128)S(1)}, f32[32]{0:T(128)S(1)}) all-reduce(f32[32]{0:T(128)S(1)} %get-tuple-element.15, f32[32]{0:T(128)S(1)} %get-tuple-element.14, f32[32]{0:T(128)S(1)} %copy-done.32, ...), channel_id=1, replica_groups=mesh['gx_0'=4,'gx_1'=2,'gy'=16,'gz'=4] {'gx_0'}, use_global_device_ids=true, to_apply=%region_16.17 | all-reduce | flops 128 | bytes 1024 | tf_op jit(solution)/shard_map/psum | solution.py:30
  103.5 8.6 %all-reduce.3 = (f32[32]{0:T(128)S(1)}, f32[32]{0:T(128)S(1)}, f32[32]{0:T(128)S(1)}, f32[32]{0:T(128)S(1)}) all-reduce(f32[32]{0:T(128)S(1)} %get-tuple-element.33, f32[32]{0:T(128)S(1)} %get-tuple-element.34, f32[32]{0:T(128)S(1)} %get-tuple-element.35, ...), channel_id=1, replica_groups=mesh['gx_0'=4,'gx_1'=2,'gy'=16,'gz'=4] {'gx_1'}, use_global_device_ids=true, to_apply=%region_17.18 | all-reduce | flops 128 | bytes 1024 | tf_op jit(solution)/shard_map/psum | solution.py:30
  112.0 26.8 %all-reduce = (f32[32]{0:T(128)S(1)}, f32[32]{0:T(128)S(1)}, f32[32]{0:T(128)S(1)}, f32[32]{0:T(128)S(1)}) all-reduce(f32[32]{0:T(128)S(1)} %get-tuple-element.37, f32[32]{0:T(128)S(1)} %get-tuple-element.38, f32[32]{0:T(128)S(1)} %get-tuple-element.39, ...), channel_id=1, replica_groups=mesh['gx_0'=4,'gx_1'=2,'gy'=16,'gz'=4] {'gy'}, use_global_device_ids=true, to_apply=%region_18.19 | all-reduce | flops 128 | bytes 1024 | tf_op jit(solution)/shard_map/psum | solution.py:30
  138.9 7.4 %all-reduce.1 = (f32[32]{0:T(128)S(1)}, f32[32]{0:T(128)S(1)}, f32[32]{0:T(128)S(1)}, f32[32]{0:T(128)S(1)}) all-reduce(f32[32]{0:T(128)S(1)} %get-tuple-element.25, f32[32]{0:T(128)S(1)} %get-tuple-element.26, f32[32]{0:T(128)S(1)} %get-tuple-element.27, ...), channel_id=1, replica_groups=mesh['gx_0'=4,'gx_1'=2,'gy'=16,'gz'=4] {'gz'}, use_global_device_ids=true, to_apply=%region_19.20 | all-reduce | flops 128 | bytes 1024 | tf_op jit(solution)/shard_map/psum | solution.py:30
  146.3 4.1 %multiply_subtract_fusion = f32[32,6,10,130]{3,1,2,0:T(8,128)} fusion(f32[32,6,10,130]{3,1,2,0:T(8,128)} %copy-done.1, f32[32,8,12,132]{3,1,2,0:T(8,128)S(1)} %pad_maximum_fusion, f32[32]{0:T(128)S(1)} %mul.415, f32[32]{0:T(128)S(1)} %get-tuple-element.43), kind=kLoop, calls=%fused_computation.37 | loop fusion | flops 748800 | bytes 2995456 | tf_op jit(solution)/shard_map/sub | solution.py:109
  150.5 4.8 %copy.122 = f32[32,6,10,130]{0,3,2,1:T(8,128)} copy(f32[32,6,10,130]{3,1,2,0:T(8,128)} %multiply_subtract_fusion) | data formatting | bytes 1996800 | tf_op jit(solution)/shard_map/reshape | solution.py:120
  155.3 4.8 %reshape.172 = f32[32,7800]{0,1:T(8,128)} reshape(f32[32,6,10,130]{0,3,2,1:T(8,128)} %copy.122) | data formatting | bytes 1996800 | tf_op jit(solution)/shard_map/reshape | solution.py:120
  160.1 3.0 %gather_fusion.7 = f32[256,32]{1,0:T(8,128)S(1)} fusion(f32[32,7800]{0,1:T(8,128)} %reshape.172, s32[1024]{0:T(1024)} %get-tuple-element.96), kind=kCustom, calls=%fused_computation.5.clone | custom fusion | bytes 66560 | tf_op jit(solution)/shard_map/jit(_take)/gather | solution.py:125
  163.1 3.0 %gather_fusion.6 = f32[256,32]{1,0:T(8,128)S(1)} fusion(f32[32,7800]{0,1:T(8,128)} %reshape.172, s32[1024]{0:T(1024)} %get-tuple-element.97), kind=kCustom, calls=%fused_computation.4.clone | custom fusion | bytes 66560 | tf_op jit(solution)/shard_map/jit(_take)/gather | solution.py:124
  166.0 3.0 %gather_fusion.5 = f32[256,32]{1,0:T(8,128)S(1)} fusion(f32[32,7800]{0,1:T(8,128)} %reshape.172, s32[1024]{0:T(1024)} %get-tuple-element.98), kind=kCustom, calls=%fused_computation.3.clone | custom fusion | bytes 66560 | tf_op jit(solution)/shard_map/jit(_take)/gather | solution.py:125
  169.0 3.0 %gather_fusion.4 = f32[256,32]{1,0:T(8,128)S(1)} fusion(f32[32,7800]{0,1:T(8,128)} %reshape.172, s32[1024]{0:T(1024)} %get-tuple-element.99), kind=kCustom, calls=%fused_computation.2.clone | custom fusion | bytes 66560 | tf_op jit(solution)/shard_map/jit(_take)/gather | solution.py:124
  172.0 3.0 %gather_fusion.3 = f32[256,32]{1,0:T(8,128)S(1)} fusion(f32[32,7800]{0,1:T(8,128)} %reshape.172, s32[1024]{0:T(1024)} %get-tuple-element.100), kind=kCustom, calls=%fused_computation.1.clone | custom fusion | bytes 66560 | tf_op jit(solution)/shard_map/jit(_take)/gather | solution.py:125
  175.0 3.0 %gather_fusion.2 = f32[256,32]{1,0:T(8,128)S(1)} fusion(f32[32,7800]{0,1:T(8,128)} %reshape.172, s32[1024]{0:T(1024)} %get-tuple-element.101), kind=kCustom, calls=%fused_computation.clone | custom fusion | bytes 66560 | tf_op jit(solution)/shard_map/jit(_take)/gather | solution.py:124
  178.7 1.1 reshape.176
  179.8 20.1 %all-to-all-start = ((f32[128,1,192]{2,1,0:T(1,128)}), f32[128,1,192]{2,1,0:T(1,128)S(1)}, u32[]{:S(2)}, u32[]{:S(2)}) async-start(f32[128,1,192]{2,1,0:T(1,128)} %reshape.176), calls=%async_computation | async-start | bytes 262144 | tf_op jit(solution)/shard_map/all_to_all | solution.py:129
  199.9 18.2 %all-to-all-done = f32[128,1,192]{2,1,0:T(1,128)S(1)} async-done(((f32[128,1,192]{2,1,0:T(1,128)}), f32[128,1,192]{2,1,0:T(1,128)S(1)}, u32[]{:S(2)}, u32[]{:S(2)}) %all-to-all-start) | async-done | bytes 98336 | tf_op jit(solution)/shard_map/all_to_all | solution.py:129
  218.6 1.0 reduce.12
  219.8 0.8 gather_fusion.1
  220.8 1.6 multiply_reduce_fusion.3
  222.7 0.8 copy.121
  223.5 0.6 stack.43
  (114 shorter events, 9.0 us)
Async XLA Ops:
  0.6 221.8 %copy-start = (f32[32,128]{1,0:T(8,128)S(1)}, f32[32,128]{1,0:T(8,128)}, u32[]{:S(2)}) copy-start(f32[32,128]{1,0:T(8,128)} %param.13) | copy-start | bytes 49156
  1.4 22.6 %collective-permute-start.6 = (s32[2,8,128]{2,1,0:T(8,128)S(1)}, s32[2,8,128]{2,1,0:T(8,128)S(1)}, u32[]{:S(2)}, u32[]{:S(2)}) collective-permute-start(s32[2,8,128]{2,1,0:T(8,128)S(1)} %get-tuple-element.70), channel_id=1, source_target_pairs={{0,64},{64,128},{128,192},{192,256},{256,320},{320,384},{384,448},... | collective-permute-start | bytes 24584 | tf_op jit(solution)/shard_map/ppermute | solution.py:20
  6.0 18.1 %collective-permute-start.7 = (s32[2,8,128]{2,1,0:T(8,128)S(1)}, s32[2,8,128]{2,1,0:T(8,128)S(1)}, u32[]{:S(2)}, u32[]{:S(2)}) collective-permute-start(s32[2,8,128]{2,1,0:T(8,128)S(1)} %get-tuple-element.71), channel_id=1, source_target_pairs={{64,0},{128,64},{192,128},{256,192},{320,256},{384,320},{448,384},... | collective-permute-start | bytes 24584 | tf_op jit(solution)/shard_map/ppermute | solution.py:23
  12.5 31.5 %collective-permute-start = (f32[32,2,8,128]{3,2,1,0:T(8,128)S(1)}, f32[32,2,8,128]{3,2,1,0:T(8,128)S(1)}, u32[]{:S(2)}, u32[]{:S(2)}) collective-permute-start(f32[32,2,8,128]{3,2,1,0:T(8,128)S(1)} %get-tuple-element.51), channel_id=1, source_target_pairs={{0,64},{64,128},{128,192},{192,256},{256,320},{320,384},{384,448},... | collective-permute-start | bytes 786440 | tf_op jit(solution)/shard_map/ppermute | solution.py:20
  14.4 29.7 %collective-permute-start.1 = (f32[32,2,8,128]{3,2,1,0:T(8,128)S(1)}, f32[32,2,8,128]{3,2,1,0:T(8,128)S(1)}, u32[]{:S(2)}, u32[]{:S(2)}) collective-permute-start(f32[32,2,8,128]{3,2,1,0:T(8,128)S(1)} %get-tuple-element.52), channel_id=1, source_target_pairs={{64,0},{128,64},{192,128},{256,192},{320,256},{384,320},{448,384},... | collective-permute-start | bytes 786440 | tf_op jit(solution)/shard_map/ppermute | solution.py:23
  24.0 3.2 %collective-permute-start.8 = (s32[8,2,128]{2,1,0:T(2,128)S(1)}, s32[8,2,128]{2,1,0:T(2,128)S(1)}, u32[]{:S(2)}, u32[]{:S(2)}) collective-permute-start(s32[8,2,128]{2,1,0:T(2,128)S(1)} %get-tuple-element.68), channel_id=1, source_target_pairs={{0,4},{4,8},{8,12},{12,16},{16,20},{20,24},{24,28},{28,32},{32,36}... | collective-permute-start | bytes 24584 | tf_op jit(solution)/shard_map/ppermute | solution.py:20
  25.3 4.5 %collective-permute-start.9 = (s32[8,2,128]{2,1,0:T(2,128)S(1)}, s32[8,2,128]{2,1,0:T(2,128)S(1)}, u32[]{:S(2)}, u32[]{:S(2)}) collective-permute-start(s32[8,2,128]{2,1,0:T(2,128)S(1)} %get-tuple-element.69), channel_id=1, source_target_pairs={{4,0},{8,4},{12,8},{16,12},{20,16},{24,20},{28,24},{32,28},{36,32}... | collective-permute-start | bytes 24584 | tf_op jit(solution)/shard_map/ppermute | solution.py:23
  30.0 5.6 %collective-permute-start.10 = (s32[8,12,2]{2,1,0:T(8,128)S(1)}, s32[8,12,2]{2,1,0:T(8,128)S(1)}, u32[]{:S(2)}, u32[]{:S(2)}) collective-permute-start(s32[8,12,2]{2,1,0:T(8,128)S(1)} %get-tuple-element.66), channel_id=1, source_target_pairs={{0,1},{1,2},{2,3},{4,5},{5,6},{6,7},{8,9},{9,10},{10,11},{12,13},{... | collective-permute-start | bytes 2312 | tf_op jit(solution)/shard_map/ppermute | solution.py:20
  33.1 5.9 %collective-permute-start.11 = (s32[8,12,2]{2,1,0:T(8,128)S(1)}, s32[8,12,2]{2,1,0:T(8,128)S(1)}, u32[]{:S(2)}, u32[]{:S(2)}) collective-permute-start(s32[8,12,2]{2,1,0:T(8,128)S(1)} %get-tuple-element.67), channel_id=1, source_target_pairs={{1,0},{2,1},{3,2},{5,4},{6,5},{7,6},{9,8},{10,9},{11,10},{13,12},{... | collective-permute-start | bytes 2312 | tf_op jit(solution)/shard_map/ppermute | solution.py:23
  35.6 23.3 %copy-start.4 = (f32[32,4,8,128]{3,1,2,0:T(4,128)}, f32[32,4,8,128]{3,1,2,0:T(4,128)S(1)}, u32[]{:S(2)}) copy-start(f32[32,4,8,128]{3,1,2,0:T(4,128)S(1)} %copy.105) | copy-start | bytes 1572868
  44.3 15.6 %copy-start.7 = (f32[32,2,8,128]{3,1,2,0:T(2,128)}, f32[32,2,8,128]{3,1,2,0:T(2,128)S(1)}, u32[]{:S(2)}) copy-start(f32[32,2,8,128]{3,1,2,0:T(2,128)S(1)} %copy.92) | copy-start | bytes 786436
  44.5 8.6 %collective-permute-start.2 = (f32[32,8,2,128]{3,1,2,0:T(8,128)S(1)}, f32[32,8,2,128]{3,1,2,0:T(8,128)S(1)}, u32[]{:S(2)}, u32[]{:S(2)}) collective-permute-start(f32[32,8,2,128]{3,1,2,0:T(8,128)S(1)} %get-tuple-element.49), channel_id=1, source_target_pairs={{0,4},{4,8},{8,12},{12,16},{16,20},{20,24},{24,28},{28,32},{32,36}... | collective-permute-start | bytes 786440 | tf_op jit(solution)/shard_map/ppermute | solution.py:20
  48.0 10.8 %collective-permute-start.3 = (f32[32,8,2,128]{3,1,2,0:T(8,128)S(1)}, f32[32,8,2,128]{3,1,2,0:T(8,128)S(1)}, u32[]{:S(2)}, u32[]{:S(2)}) collective-permute-start(f32[32,8,2,128]{3,1,2,0:T(8,128)S(1)} %get-tuple-element.50), channel_id=1, source_target_pairs={{4,0},{8,4},{12,8},{16,12},{20,16},{24,20},{28,24},{32,28},{36,32}... | collective-permute-start | bytes 786440 | tf_op jit(solution)/shard_map/ppermute | solution.py:23
  53.1 5.7 %copy-start.9 = (f32[32,8,2,128]{3,1,2,0:T(8,128)}, f32[32,8,2,128]{3,1,2,0:T(8,128)S(1)}, u32[]{:S(2)}) copy-start(f32[32,8,2,128]{3,1,2,0:T(8,128)S(1)} %collective-permute-done.2) | copy-start | bytes 786436
  58.8 0.7 copy-start.11
  61.6 9.1 %copy-start.25 = (f32[4,8,128]{2,1,0:T(8,128)S(1)}, f32[4,8,128]{2,1,0:T(8,128)}, u32[]{:S(2)}) copy-start(f32[4,8,128]{2,1,0:T(8,128)} %get-tuple-element.58) | copy-start | bytes 49156
  61.6 9.1 %copy-start.24 = (f32[4,8,128]{2,1,0:T(8,128)S(1)}, f32[4,8,128]{2,1,0:T(8,128)}, u32[]{:S(2)}) copy-start(f32[4,8,128]{2,1,0:T(8,128)} %get-tuple-element.53) | copy-start | bytes 49156
  61.6 9.7 %copy-start.23 = (f32[4,8,128]{2,1,0:T(8,128)S(1)}, f32[4,8,128]{2,1,0:T(8,128)}, u32[]{:S(2)}) copy-start(f32[4,8,128]{2,1,0:T(8,128)} %get-tuple-element.54) | copy-start | bytes 49156
  61.6 10.3 %copy-start.22 = (f32[4,8,128]{2,1,0:T(8,128)S(1)}, f32[4,8,128]{2,1,0:T(8,128)}, u32[]{:S(2)}) copy-start(f32[4,8,128]{2,1,0:T(8,128)} %get-tuple-element.55) | copy-start | bytes 49156
  64.7 14.2 %collective-permute-start.5 = (f32[32,8,12,2]{0,1,3,2:T(8,128)S(1)}, f32[32,8,12,2]{0,1,3,2:T(8,128)S(1)}, u32[]{:S(2)}, u32[]{:S(2)}) collective-permute-start(f32[32,8,12,2]{0,1,3,2:T(8,128)S(1)} %copy.94), channel_id=1, source_target_pairs={{1,0},{2,1},{3,2},{5,4},{6,5},{7,6},{9,8},{10,9},{11,10},{13,12},{... | collective-permute-start | bytes 73736 | tf_op jit(solution)/shard_map/ppermute | solution.py:23
  66.0 10.5 %collective-permute-start.4 = (f32[32,8,12,2]{0,1,3,2:T(8,128)S(1)}, f32[32,8,12,2]{0,1,3,2:T(8,128)S(1)}, u32[]{:S(2)}, u32[]{:S(2)}) collective-permute-start(f32[32,8,12,2]{0,1,3,2:T(8,128)S(1)} %copy.93), channel_id=1, source_target_pairs={{0,1},{1,2},{2,3},{4,5},{5,6},{6,7},{8,9},{9,10},{10,11},{12,13},{... | collective-permute-start | bytes 73736 | tf_op jit(solution)/shard_map/ppermute | solution.py:20
  81.3 4.9 %copy-start.2 = (f32[32,8,12,2]{3,1,2,0:T(8,128)S(1)}, f32[32,8,12,2]{3,1,2,0:T(8,128)}, u32[]{:S(2)}) copy-start(f32[32,8,12,2]{3,1,2,0:T(8,128)} %copy.95) | copy-start | bytes 73732
  81.3 4.9 %copy-start.3 = (f32[32,8,12,2]{3,1,2,0:T(8,128)S(1)}, f32[32,8,12,2]{3,1,2,0:T(8,128)}, u32[]{:S(2)}) copy-start(f32[32,8,12,2]{3,1,2,0:T(8,128)} %copy.96) | copy-start | bytes 73732
  81.3 4.9 %copy-start.5 = (f32[32,4,8,128]{3,1,2,0:T(4,128)S(1)}, f32[32,4,8,128]{3,1,2,0:T(4,128)}, u32[]{:S(2)}) copy-start(f32[32,4,8,128]{3,1,2,0:T(4,128)} %copy-done.4) | copy-start | bytes 1572868
  81.3 4.9 %copy-start.8 = (f32[32,2,8,128]{3,1,2,0:T(2,128)S(1)}, f32[32,2,8,128]{3,1,2,0:T(2,128)}, u32[]{:S(2)}) copy-start(f32[32,2,8,128]{3,1,2,0:T(2,128)} %copy-done.7) | copy-start | bytes 786436
  81.3 4.9 %copy-start.10 = (f32[32,8,2,128]{3,1,2,0:T(8,128)S(1)}, f32[32,8,2,128]{3,1,2,0:T(8,128)}, u32[]{:S(2)}) copy-start(f32[32,8,2,128]{3,1,2,0:T(8,128)} %copy-done.9) | copy-start | bytes 786436
  81.3 4.9 %copy-start.12 = (f32[32,8,2,128]{3,1,2,0:T(8,128)S(1)}, f32[32,8,2,128]{3,1,2,0:T(8,128)}, u32[]{:S(2)}) copy-start(f32[32,8,2,128]{3,1,2,0:T(8,128)} %copy-done.11) | copy-start | bytes 786436
  81.3 4.9 %copy-start.13 = (f32[6,10,130]{2,0,1:T(8,128)S(1)}, f32[6,10,130]{2,0,1:T(8,128)}, u32[]{:S(2)}) copy-start(f32[6,10,130]{2,0,1:T(8,128)} %copy.98) | copy-start | bytes 93604
  81.3 4.9 %copy-start.14 = (f32[6,10,130]{2,0,1:T(8,128)S(1)}, f32[6,10,130]{2,0,1:T(8,128)}, u32[]{:S(2)}) copy-start(f32[6,10,130]{2,0,1:T(8,128)} %copy.99) | copy-start | bytes 93604
  81.4 4.9 %copy-start.15 = (f32[6,10,130]{2,0,1:T(8,128)S(1)}, f32[6,10,130]{2,0,1:T(8,128)}, u32[]{:S(2)}) copy-start(f32[6,10,130]{2,0,1:T(8,128)} %copy.97) | copy-start | bytes 93604
  81.4 4.9 %copy-start.16 = (f32[6,10,130]{2,0,1:T(8,128)S(1)}, f32[6,10,130]{2,0,1:T(8,128)}, u32[]{:S(2)}) copy-start(f32[6,10,130]{2,0,1:T(8,128)} %copy.101) | copy-start | bytes 93604
  81.4 4.9 %copy-start.17 = (f32[6,10,130]{2,0,1:T(8,128)S(1)}, f32[6,10,130]{2,0,1:T(8,128)}, u32[]{:S(2)}) copy-start(f32[6,10,130]{2,0,1:T(8,128)} %copy.100) | copy-start | bytes 93604
  86.3 8.8 %copy-start.6 = (f32[32,4,8,128]{3,2,1,0:T(8,128)S(1)}, f32[32,4,8,128]{3,2,1,0:T(8,128)}, u32[]{:S(2)}) copy-start(f32[32,4,8,128]{3,2,1,0:T(8,128)} %param.8) | copy-start | bytes 1572868
  86.3 8.8 %copy-start.18 = (f32[4,8,128]{2,0,1:T(4,128)S(1)}, f32[4,8,128]{2,0,1:T(4,128)}, u32[]{:S(2)}) copy-start(f32[4,8,128]{2,0,1:T(4,128)} %copy.106) | copy-start | bytes 49156
  86.3 8.8 %copy-start.19 = (f32[4,8,128]{2,0,1:T(4,128)S(1)}, f32[4,8,128]{2,0,1:T(4,128)}, u32[]{:S(2)}) copy-start(f32[4,8,128]{2,0,1:T(4,128)} %copy.109) | copy-start | bytes 49156
  86.3 8.8 %copy-start.20 = (f32[4,8,128]{2,0,1:T(4,128)S(1)}, f32[4,8,128]{2,0,1:T(4,128)}, u32[]{:S(2)}) copy-start(f32[4,8,128]{2,0,1:T(4,128)} %copy.108) | copy-start | bytes 49156
  86.3 8.7 %copy-start.21 = (f32[4,8,128]{2,0,1:T(4,128)S(1)}, f32[4,8,128]{2,0,1:T(4,128)}, u32[]{:S(2)}) copy-start(f32[4,8,128]{2,0,1:T(4,128)} %copy.107) | copy-start | bytes 49156
  93.6 1.5 copy-start.1
  95.1 2.4 %copy-start.32 = (f32[32]{0:T(128)S(1)}, f32[32]{0:T(128)}, u32[]{:S(2)}) copy-start(f32[32]{0:T(128)} %multiply_reduce_fusion.2) | copy-start | bytes 388
  155.2 22.8 %copy-start.26 = (f32[256]{0:T(256)S(1)}, f32[256]{0:T(256)}, u32[]{:S(2)}) copy-start(f32[256]{0:T(256)} %select_multiply_fusion) | copy-start | bytes 3076
  155.2 22.8 %copy-start.27 = (pred[256]{0:T(512)(128)(4,1)S(1)}, pred[256]{0:T(512)(128)(4,1)}, u32[]{:S(2)}) copy-start(pred[256]{0:T(512)(128)(4,1)} %get-tuple-element.75) | copy-start | bytes 772
  155.2 22.8 %copy-start.28 = (pred[256]{0:T(512)(128)(4,1)S(1)}, pred[256]{0:T(512)(128)(4,1)}, u32[]{:S(2)}) copy-start(pred[256]{0:T(512)(128)(4,1)} %get-tuple-element.76) | copy-start | bytes 772
  155.2 22.8 %copy-start.29 = (pred[256]{0:T(512)(128)(4,1)S(1)}, pred[256]{0:T(512)(128)(4,1)}, u32[]{:S(2)}) copy-start(pred[256]{0:T(512)(128)(4,1)} %get-tuple-element.77) | copy-start | bytes 772
  155.3 22.8 %copy-start.30 = (pred[256]{0:T(512)(128)(4,1)S(1)}, pred[256]{0:T(512)(128)(4,1)}, u32[]{:S(2)}) copy-start(pred[256]{0:T(512)(128)(4,1)} %get-tuple-element.78) | copy-start | bytes 772
  155.3 22.8 %copy-start.31 = (pred[256]{0:T(512)(128)(4,1)S(1)}, pred[256]{0:T(512)(128)(4,1)}, u32[]{:S(2)}) copy-start(pred[256]{0:T(512)(128)(4,1)} %get-tuple-element.79) | copy-start | bytes 772
  155.3 22.8 %copy-start.33 = (pred[256]{0:T(512)(128)(4,1)S(1)}, pred[256]{0:T(512)(128)(4,1)}, u32[]{:S(2)}) copy-start(pred[256]{0:T(512)(128)(4,1)} %get-tuple-element.41) | copy-start | bytes 772
  163.0 36.8 %copy-start.34 = (s32[128]{0:T(128)S(1)}, s32[128]{0:T(128)}, u32[]{:S(2)}) copy-start(s32[128]{0:T(128)} %param.12) | copy-start | bytes 1540
  179.8 38.3 %all-to-all-start = ((f32[128,1,192]{2,1,0:T(1,128)}), f32[128,1,192]{2,1,0:T(1,128)S(1)}, u32[]{:S(2)}, u32[]{:S(2)}) async-start(f32[128,1,192]{2,1,0:T(1,128)} %reshape.176), calls=%async_computation | async-start | bytes 262144 | tf_op jit(solution)/shard_map/all_to_all | solution.py:129
where the time goes:
time: 225 us; the launch traced here: 224 us
  local copies, waits for them, and re-layouts  55.3 us (25%)
  starting transfers between devices  51.7 us (23%)
  blocking collectives  48.8 us (22%)
  other arithmetic  35.7 us (16%)
  waiting for transfers between devices  31 us (14%)
    psum x4, blocking collectives, by_axis(): x = lax.psum(x, axis)  48.8 us
    all_to_all x1, starting transfers between devices, per_device(): lax.all_to_all(columns, GX_GY, split_axis=2, concat_axis=2, tiled=True)  20.1 us
    ppermute x6, starting transfers between devices, extended(): lax.ppermute(lax.slice_in_dim(block, block.shape[dim] - width, None, axis...  18.6 us
    all_to_all x1, waiting for transfers between devices, per_device(): lax.all_to_all(columns, GX_GY, split_axis=2, concat_axis=2, tiled=True)  18.2 us
    ppermute x6, starting transfers between devices, extended(): lax.ppermute(lax.slice_in_dim(block, 0, width, axis=dim), axis, backward)  13 us
    ppermute x6, waiting for transfers between devices, extended(): lax.ppermute(lax.slice_in_dim(block, 0, width, axis=dim), axis, backward)  11.7 us
    reshape x2, local copies, waits for them, and re-layouts, per_device(): flattened = solution_pad.reshape(sensors, -1)  9.55 us
    gather x3, local copies, waits for them, and re-layouts, gradient(): upper = jnp.take(flattened, centre + stride, axis=1)  8.97 us
  transfers between devices with their start and end apart: 13, of which 5 were waited for; matrix products, arithmetic and copies ran while one was open for 12% of the time, Pallas kernels for 0%

commit v1 on v0

v1 whole, which is shorter than its diff:
```python
import functools

import jax
import jax.numpy as jnp
from jax import lax
from jax.experimental import pallas as pl
from jax.experimental.pallas import tpu as pltpu
from jax.sharding import PartitionSpec as P

F32 = jnp.float32
BF16 = jnp.bfloat16
MASS = 0.25
PAIRS = ((0, 0), (1, 1), (2, 2), (0, 1), (0, 2), (1, 2))
AXES = ("gx", "gy", "gz")


class Exchange:
    def __init__(self, send, recv):
        self.send, self.recv, self.used = send, recv, 0

    def start(self, source, target, axis, partner):
        copy = pltpu.make_async_remote_copy(
            src_ref=source,
            dst_ref=target,
            send_sem=self.send.at[self.used],
            recv_sem=self.recv.at[self.used],
            device_id={axis: partner},
            device_id_type=pl.DeviceIdType.MESH,
        )
        self.used += 1
        copy.start()
        return copy


def copies_needed(sizes):
    lines = sum(n - 1 for n in sizes)
    return 18 + lines + 2 * (sizes[0] - 1) + 2 * (sizes[1] - 1)


def kernel(sizes, src, lab, table, send_map, slots, data, proj, gram,
           field, image, xr_b, xr_v, ys_b, ys_v, yr_b, yr_v, zs_b, zs_v, zr_b, zr_v, zm,
           lys, lxr, lyr, lzr, wts, ghi, glo, onehot, pick, raw, turned,
           line_b, line_v, mid_b, mid_v, out_b, out_v, fin_b, fin_v, mq, red_x, red_y, red_z,
           load_sem, send_sem, recv_sem):
    nx, ny, nz = sizes
    count = dict(zip(AXES, sizes))
    me = {axis: lax.axis_index(axis) for axis in AXES}
    low = {axis: lax.rem(me[axis] + count[axis] - 1, count[axis]) for axis in AXES}
    high = {axis: lax.rem(me[axis] + 1, count[axis]) for axis in AXES}
    has_low = {axis: me[axis] > 0 for axis in AXES}
    has_high = {axis: me[axis] < count[axis] - 1 for axis in AXES}
    keep_low = {axis: jnp.where(has_low[axis], 1.0, 0.0).astype(F32) for axis in AXES}
    keep_high = {axis: jnp.where(has_high[axis], 1.0, 0.0).astype(F32) for axis in AXES}
    sensors, cells_xy, lanes = field.shape
    cx, cy = cells_xy // 8, 8
    cap = send_map.shape[1] // (nx * ny)
    total_slots = send_map.shape[1]
    ex = Exchange(send_sem, recv_sem)
    lane = lax.broadcasted_iota(jnp.int32, (8, lanes), 1)
    row = lax.broadcasted_iota(jnp.int32, (8, lanes), 0)

    load = pltpu.make_async_copy(src, field, load_sem)
    load.start()
    barrier = pltpu.get_barrier_semaphore()
    for axis in AXES:
        for d in range(1, count[axis]):
            partner = lax.rem(me[axis] + d, count[axis])
            pl.semaphore_signal(
                barrier, inc=1, device_id={axis: partner}, device_id_type=pl.DeviceIdType.MESH
            )
    lys[0:cx, :] = lab[pl.ds(0, cx, stride=cy), :]
    lys[cx : 2 * cx, :] = lab[pl.ds(cy - 1, cx, stride=cy), :]
    load.wait()

    def pack(whole, ys, zs):
        for s in range(sensors):
            for side, y in enumerate((0, cy - 1)):
                ys[side, cx * s : cx * s + cx, :] = whole[s, pl.ds(y, cx, stride=cy), :]

        def one(s, acc):
            here = lax.shift_right_logical(lane, 1) == s
            return tuple(
                jnp.where(here, pltpu.roll(whole[s, 8 * x : 8 * x + 8, :], 2 * s + 1, 1), acc[x])
                for x in range(cx)
            )

        acc = lax.fori_loop(0, sensors, one, (jnp.zeros((8, lanes), F32),) * cx, unroll=4)
        for x in range(cx):
            zs[8 * x : 8 * x + 8, :] = acc[x]

    def faces(whole, xr, ys, yr, zs, zr):
        last = cells_xy - 8
        return [
            ex.start(whole.at[:, 0:8, :], xr.at[1], "gx", low["gx"]),
            ex.start(whole.at[:, last : last + 8, :], xr.at[0], "gx", high["gx"]),
            ex.start(ys.at[0], yr.at[1], "gy", low["gy"]),
            ex.start(ys.at[1], yr.at[0], "gy", high["gy"]),
            ex.start(zs, zr.at[1], "gz", low["gz"]),
            ex.start(zs, zr.at[0], "gz", high["gz"]),
        ]

    pack(field, ys_b, zs_b)
    pl.semaphore_wait(barrier, sum(n - 1 for n in sizes))
    label_copies = [
        ex.start(lab.at[0:8, :], lxr.at[1], "gx", low["gx"]),
        ex.start(lab.at[cells_xy - 8 : cells_xy, :], lxr.at[0], "gx", high["gx"]),
        ex.start(lys, lyr.at[1], "gy", low["gy"]),
        ex.start(lys, lyr.at[0], "gy", high["gy"]),
        ex.start(lab, lzr.at[1], "gz", low["gz"]),
        ex.start(lab, lzr.at[0], "gz", high["gz"]),
    ]
    first_copies = faces(field, xr_b, ys_b, yr_b, zs_b, zr_b)

    wanted = send_map[...]
    key = lax.shift_right_arithmetic(wanted, 10) * lanes + (wanted & (lanes - 1))
    y_of = lax.shift_right_arithmetic(wanted, 7) & (cy - 1)
    for x in range(cx):
        places = lax.broadcasted_iota(jnp.int32, (lanes, total_slots), 0) + x * lanes
        onehot[x * lanes : (x + 1) * lanes, :] = jnp.where(places == key, 1.0, 0.0).astype(BF16)
    rows_in = lax.broadcasted_iota(jnp.int32, (total_slots, slots.shape[1]), 0)
    pick[...] = jnp.where(rows_in == slots[...], 1.0, 0.0).astype(BF16)

    for copy in label_copies:
        copy.wait()

    def tissue(shifted):
        level = jnp.zeros(shifted.shape, F32)
        for k in range(table.shape[0]):
            level = level + jnp.where(shifted == k + 1, table[k], 0.0)
        return level, jnp.where(shifted > 0, 1.0, 0.0).astype(F32)

    shifted = [lab[8 * x : 8 * x + 8, :] + 1 for x in range(cx)]
    for x in range(cx):
        here = shifted[x]
        if x > 0:
            x_low = shifted[x - 1]
        else:
            x_low = jnp.where(has_low["gx"], lxr[0] + 1, 0)
        if x < cx - 1:
            x_high = shifted[x + 1]
        else:
            x_high = jnp.where(has_high["gx"], lxr[1] + 1, 0)
        row_low = jnp.where(has_low["gy"], lyr[0, cx + x : cx + x + 1, :] + 1, 0)
        row_high = jnp.where(has_high["gy"], lyr[1, x : x + 1, :] + 1, 0)
        y_low = jnp.where(row == 0, row_low, pltpu.roll(here, 1, 0))
        y_high = jnp.where(row == cy - 1, row_high, pltpu.roll(here, cy - 1, 0))
        side_low = jnp.where(has_low["gz"], lzr[0, 8 * x : 8 * x + 8, :] + 1, 0)
        side_high = jnp.where(has_high["gz"], lzr[1, 8 * x : 8 * x + 8, :] + 1, 0)
        z_low = pltpu.roll(jnp.where(lane == lanes - 1, side_low, here), 1, 1)
        z_high = pltpu.roll(jnp.where(lane == 0, side_high, here), lanes - 1, 1)
        own_cond, own_in = tissue(here)
        diagonal = jnp.full((8, lanes), MASS, F32)
        for k, beside in enumerate((x_low, x_high, y_low, y_high, z_low, z_high)):
            its_cond, its_in = tissue(beside)
            weight = 0.5 * (own_cond + its_cond) * own_in * its_in
            wts[k, 8 * x : 8 * x + 8, :] = weight
            diagonal = diagonal + weight
        wts[6, 8 * x : 8 * x + 8, :] = diagonal
        wts[7, 8 * x : 8 * x + 8, :] = 0.5 * own_cond

    def sweep(whole, xr, yr, zr, result):
        for x in range(cx):
            span = slice(8 * x, 8 * x + 8)
            zm[span, :] = jnp.where(
                (lane & 1) == 0, zr[0, span, :] * keep_low["gz"], zr[1, span, :] * keep_high["gz"]
            )

        def pair(i, carry):
            slopes = [[[None, None] for _ in range(cx)] for _ in range(3)]
            for k in range(2):
                s = 2 * i + k
                own = [whole[s, 8 * x : 8 * x + 8, :] for x in range(cx)]
                outer = [xr[0, s] * keep_low["gx"]] + own + [xr[1, s] * keep_high["gx"]]
                sums = [None, None, None]
                for x in range(cx):
                    span = slice(8 * x, 8 * x + 8)
                    u = own[x]
                    low_row = yr[0, pl.ds(s * cx + x, 1), :] * keep_low["gy"]
                    high_row = yr[1, pl.ds(s * cx + x, 1), :] * keep_high["gy"]
                    y_low = jnp.where(row == 0, low_row, pltpu.roll(u, 1, 0))
                    y_high = jnp.where(row == cy - 1, high_row, pltpu.roll(u, cy - 1, 0))
                    beyond = pltpu.roll(zm[span, :], lanes - 1 - 2 * s, 1)
                    z_low = pltpu.roll(jnp.where(lane == lanes - 1, beyond, u), 1, 1)
                    z_high = pltpu.roll(jnp.where(lane == 0, beyond, u), lanes - 1, 1)
                    near = (outer[x], outer[x + 2], y_low, y_high, z_low, z_high)
                    q = wts[6, span, :] * u
                    for n in range(6):
                        q = q - wts[n, span, :] * near[n]
                    half = wts[7, span, :]
                    for c in range(3):
                        slopes[c][x][k] = half * (near[2 * c + 1] - near[2 * c])
                    if result is not None:
                        result[s, span, :] = q
                        terms = (u * u, u * q, q * q)
                    else:
                        terms = (u * q,)
                    for n, term in enumerate(terms):
                        sums[n] = term if sums[n] is None else sums[n] + term
                first = 0 if result is not None else 3
                for n in range(3 if result is not None else 1):
                    mq[first + n, pl.ds(pl.multiple_of(8 * s, 8), 8), :] = sums[n]
            at = pl.ds(pl.multiple_of(16 * i, 16), 16)
            for c in range(3):
                for x in range(cx):
                    slope = jnp.concatenate(slopes[c][x], axis=0)
                    coarse = slope.astype(BF16)
                    ghi[c, at, x * lanes : (x + 1) * lanes] = coarse
                    glo[c, at, x * lanes : (x + 1) * lanes] = (slope - coarse.astype(F32)).astype(BF16)
            return carry

        lax.fori_loop(0, sensors // 2, pair, 0)

    def gather(line):
        parts = []
        for c in range(3):
            product = jnp.dot(ghi[c], onehot[...], preferred_element_type=F32) + jnp.dot(
                glo[c], onehot[...], preferred_element_type=F32
            )
            for h in range(total_slots // lanes):
                raw[h] = product[:, h * lanes : (h + 1) * lanes]
            for g in range(sensors // 8):
                halves = []
                for h in range(total_slots // lanes):
                    acc = None
                    for y in range(cy):
                        strip = raw[h, pl.ds(8 * cy * g + y, 8, stride=cy), :]
                        term = jnp.where(y_of[:, h * lanes : (h + 1) * lanes] == y, strip, 0.0)
                        acc = term if acc is None else acc + term
                    halves.append(acc)
                parts.append(jnp.concatenate(halves, axis=1))
        parts.append(jnp.zeros((lanes - 3 * sensors, total_slots), F32))
        turned[...] = jnp.concatenate(parts, axis=0).T
        for j in range(ny * cap):
            line[j * nx : (j + 1) * nx, :] = turned[pl.ds(j, nx, stride=ny * cap), :]

    def spread(source, target, axis):
        rows = source.shape[0] // count[axis]
        mine = pl.ds(pl.multiple_of(me[axis] * rows, rows), rows)
        copies = []
        for d in range(1, count[axis]):
            partner = lax.rem(me[axis] + d, count[axis])
            theirs = pl.ds(pl.multiple_of(partner * rows, rows), rows)
            copies.append(ex.start(source.at[theirs, :], target.at[mine, :], axis, partner))
        target[mine, :] = source[mine, :]
        return copies

    def regroup(mid, out):
        rows = ny * cap
        for ix in range(nx):
            out[ix * rows : (ix + 1) * rows, :] = mid[pl.ds(ix, rows, stride=nx), :]

    def reduce_start(buffer, value, axis):
        buffer[0] = value
        copies = []
        for d in range(1, count[axis]):
            partner = lax.rem(me[axis] + d, count[axis])
            copies.append(ex.start(buffer.at[0], buffer.at[d], axis, partner))
        return copies

    def reduce_end(buffer, copies):
        for copy in copies:
            copy.wait()
        value = buffer[0]
        for d in range(1, len(copies) + 1):
            value = value + buffer[d]
        return value

    for copy in first_copies:
        copy.wait()
    sweep(field, xr_b, yr_b, zr_b, image)
    pack(image, ys_v, zs_v)
    second_copies = faces(image, xr_v, ys_v, yr_v, zs_v, zr_v)
    gather(line_b)
    line_b_copies = spread(line_b, mid_b, "gy")
    for copy in second_copies:
        copy.wait()
    sweep(image, xr_v, yr_v, zr_v, None)

    rows = []
    for m in range(4):
        for g in range(sensors // 8):
            acc = None
            for y in range(cy):
                strip = mq[m, pl.ds(8 * cy * g + y, 8, stride=cy), :]
                acc = strip if acc is None else acc + strip
            rows.append(acc)
    partial = lax.dot_general(
        jnp.ones((8, lanes), F32),
        jnp.concatenate(rows, axis=0),
        (((1,), (1,)), ((), ())),
        precision=lax.Precision.HIGHEST,
        preferred_element_type=F32,
    )[0:1, :]
    z_copies = reduce_start(red_z, partial, "gz")
    gather(line_v)
    line_v_copies = spread(line_v, mid_v, "gy")
    x_copies = reduce_start(red_x, reduce_end(red_z, z_copies), "gx")
    for copy in line_b_copies:
        copy.wait()
    regroup(mid_b, out_b)
    out_b_copies = spread(out_b, fin_b, "gx")
    y_copies = reduce_start(red_y, reduce_end(red_x, x_copies), "gy")
    for copy in line_v_copies:
        copy.wait()
    regroup(mid_v, out_v)
    out_v_copies = spread(out_v, fin_v, "gx")

    moments = jnp.broadcast_to(reduce_end(red_y, y_copies), (8, lanes))
    group = lane // sensors
    full = []
    for m in range(4):
        value = moments
        for g in range(lanes // sensors):
            shift = (sensors * (g - m)) % lanes
            turn = pltpu.roll(moments, shift, 1) if shift else moments
            value = jnp.where(group == g, turn, value)
        full.append(value)
    zero, one, two, three = full
    first_step = zero / one
    residue = first_step * first_step * two - zero
    growth = 1.0 + residue / zero
    curvature = growth * growth * one - 2.0 * growth * first_step * two + first_step * first_step * three
    second_step = residue / curvature
    source_coef = (first_step + second_step * growth)[0:1, :]
    image_coef = (second_step * first_step)[0:1, :]

    for copy in out_b_copies + out_v_copies:
        copy.wait()
    columns = (source_coef * fin_b[...] - image_coef * fin_v[...]).T
    coarse = columns.astype(BF16)
    fine = (columns - coarse.astype(F32)).astype(BF16)
    owned = jnp.dot(coarse, pick[...], preferred_element_type=F32) + jnp.dot(
        fine, pick[...], preferred_element_type=F32
    )
    per_time = data[...].T
    parts = [owned[sensors * c : sensors * (c + 1), :] for c in range(3)]
    for c in range(3):
        proj[c] = jnp.dot(
            per_time, parts[c], precision=lax.Precision.HIGHEST, preferred_element_type=F32
        )
    for k, (a, b) in enumerate(PAIRS):
        gram[k : k + 1, :] = jnp.sum(parts[a] * parts[b], axis=0, keepdims=True)


def per_device(sizes, source_term, labels, table, send_map, owner_slots, sensor_data):
    sensors, cx, cy, lanes = source_term.shape
    cells_xy = cx * cy
    total = send_map.shape[-1]
    owned = owner_slots.shape[0]
    times = sensor_data.shape[1]
    n = copies_needed(sizes)
    vmem = pltpu.VMEM
    scratch = [
        vmem((sensors, cells_xy, lanes), F32),
        vmem((sensors, cells_xy, lanes), F32),
        vmem((2, sensors, 8, lanes), F32),
        vmem((2, sensors, 8, lanes), F32),
        vmem((2, sensors * cx, lanes), F32),
        vmem((2, sensors * cx, lanes), F32),
        vmem((2, sensors * cx, lanes), F32),
        vmem((2, sensors * cx, lanes), F32),
        vmem((cells_xy, lanes), F32),
        vmem((cells_xy, lanes), F32),
        vmem((2, cells_xy, lanes), F32),
        vmem((2, cells_xy, lanes), F32),
        vmem((cells_xy, lanes), F32),
        vmem((2 * cx, lanes), jnp.int32),
        vmem((2, 8, lanes), jnp.int32),
        vmem((2, 2 * cx, lanes), jnp.int32),
        vmem((2, cells_xy, lanes), jnp.int32),
        vmem((8, cells_xy, lanes), F32),
        vmem((3, sensors * 8, cx * lanes), BF16),
        vmem((3, sensors * 8, cx * lanes), BF16),
        vmem((cx * lanes, total), BF16),
        vmem((total, owned), BF16),
        vmem((total // lanes, sensors * 8, lanes), F32),
        vmem((total, lanes), F32),
    ]
    scratch += [vmem((total, lanes), F32)] * 8
    scratch += [
        vmem((4, sensors * 8, lanes), F32),
        vmem((sizes[0], 1, lanes), F32),
        vmem((sizes[1], 1, lanes), F32),
        vmem((sizes[2], 1, lanes), F32),
        pltpu.SemaphoreType.DMA,
        pltpu.SemaphoreType.DMA((n,)),
        pltpu.SemaphoreType.DMA((n,)),
    ]
    whole = pl.BlockSpec(memory_space=pltpu.VMEM)
    return pl.pallas_call(
        functools.partial(kernel, sizes),
        out_shape=(
            jax.ShapeDtypeStruct((3, times, owned), F32),
            jax.ShapeDtypeStruct((len(PAIRS), owned), F32),
        ),
        in_specs=[
            pl.BlockSpec(memory_space=pl.ANY),
            whole,
            pl.BlockSpec(memory_space=pltpu.SMEM),
            whole,
            whole,
            whole,
        ],
        out_specs=(whole, whole),
        scratch_shapes=scratch,
        compiler_params=pltpu.CompilerParams(
            collective_id=0, has_side_effects=True, vmem_limit_bytes=40 * 1024 * 1024
        ),
        name="solve",
    )(
        source_term.reshape(sensors, cells_xy, lanes),
        labels.reshape(cells_xy, lanes),
        table,
        send_map.reshape(1, total),
        owner_slots.reshape(1, owned),
        sensor_data,
    )


def solution(mesh):
    sizes = tuple(mesh.shape[axis] for axis in AXES)
    in_specs = (
        P(None, "gx", "gy", "gz"),
        P("gx", "gy", "gz"),
        P(),
        P("gx", "gy", "gz", None),
        P(AXES),
        P(),
    )
    out_specs = (P(None, None, AXES), P(None, AXES))
    return jax.shard_map(
        functools.partial(per_device, sizes),
        mesh=mesh,
        in_specs=in_specs,
        out_specs=out_specs,
        check_vma=False,
    )
```

time: 225 us -> 56 us (0.25)
  starting transfers between devices: 51.7 us -> 0 us
  local copies, waits for them, and re-layouts: 55.3 us -> 4.42 us
  Pallas kernels: 0 us -> 50.6 us
  blocking collectives: 48.8 us -> 0 us
  other arithmetic: 35.7 us -> 0 us
  waiting for transfers between devices: 31 us -> 0 us
    pallas_call x0 -> x1, Pallas kernels: none -> 50.6 us  [per_device(): pl.pallas_call(functools.partial(kernel, sizes), out_shape=(jax.ShapeDtyp...]
    psum x4 -> x0, blocking collectives: 48.8 us -> none  [by_axis(): x = lax.psum(x, axis)]
    ppermute x12 -> x0, starting transfers between devices: 31.6 us -> none  [the longest x6 18.6 us: extended(): lax.ppermute(lax.slice_in_dim(block, block.shape[dim] - width, None, axis...]
    gather x8 -> x0, local copies, waits for them, and re-layouts: 20.4 us -> none  [the longest x3 8.97 us: gradient(): upper = jnp.take(flattened, centre + stride, axis=1)]
    all_to_all x1 -> x0, starting transfers between devices: 20.1 us -> none  [per_device(): lax.all_to_all(columns, GX_GY, split_axis=2, concat_axis=2, tiled=True)]
    all_to_all x1 -> x0, waiting for transfers between devices: 18.2 us -> none  [per_device(): lax.all_to_all(columns, GX_GY, split_axis=2, concat_axis=2, tiled=True)]
    ppermute x12 -> x0, waiting for transfers between devices: 12.8 us -> none  [the longest x6 11.7 us: extended(): lax.ppermute(lax.slice_in_dim(block, 0, width, axis=dim), axis, backward)]
    add x5 -> x0, other arithmetic: 11.9 us -> none  [the longest x1 7.22 us: stencil(): accumulated = accumulated + weight * (centre - padded[leading + beside_all])]
  transfers between devices with their start and end apart: 13 -> 0, of which waited for: 5 -> 0; matrix products, arithmetic and copies ran while one was open for 12% -> 0% of each run, Pallas kernels for 0% -> 0%
where the time goes in v1:
time: 56 us; the launch traced here: 55.7 us
  Pallas kernels  50.6 us (90%)
  local copies, waits for them, and re-layouts  4.42 us (8%)
  between operations  0.67 us (1%)
    pallas_call x1, Pallas kernels, per_device(): pl.pallas_call(functools.partial(kernel, sizes), out_shape=(jax.ShapeDtyp...  50.6 us
    unnamed x14, local copies, waits for them, and re-layouts  4.42 us

profile of v1, /device:TPU:1, one launch (start us, length us, event | category | flops | bytes accessed | tf_op | source)
XLA Modules:
  0.0 55.7 jit_solution(17275119985690811899)
XLA Ops:
  0.6 0.0 copy-start.5
  0.6 0.0 copy-start.3
  0.7 0.0 copy-start.4
  0.7 0.6 %copy-done.5 = s32[128]{0:T(128)S(1)} copy-done((s32[128]{0:T(128)S(1)}, s32[128]{0:T(128)}, u32[]{:S(2)}) %copy-start.5) | copy-done | bytes 536
  1.3 0.0 copy-done.3
  1.3 0.0 copy-done.4
  1.3 0.0 copy-start
  1.3 1.0 %copy-done = f32[32,4,8,128]{3,2,1,0:T(8,128)S(1)} copy-done((f32[32,4,8,128]{3,2,1,0:T(8,128)S(1)}, f32[32,4,8,128]{3,2,1,0:T(8,128)}, u32[]{:S(2)}) %copy-start) | copy-done | bytes 524312
  2.4 0.0 copy-start.1
  2.4 0.7 %copy-done.1 = s32[4,8,128]{2,1,0:T(8,128)S(1)} copy-done((s32[4,8,128]{2,1,0:T(8,128)S(1)}, s32[4,8,128]{2,1,0:T(8,128)}, u32[]{:S(2)}) %copy-start.1) | copy-done | bytes 16408
  3.1 0.0 copy-start.2
  3.1 0.7 %copy-done.2 = f32[32,128]{1,0:T(8,128)S(1)} copy-done((f32[32,128]{1,0:T(8,128)S(1)}, f32[32,128]{1,0:T(8,128)}, u32[]{:S(2)}) %copy-start.2) | copy-done | bytes 16408
  3.8 50.6 %solve.1 = (f32[3,128,128]{2,1,0:T(8,128)S(1)}, f32[6,128]{1,0:T(8,128)S(1)}) custom-call(f32[32,32,128]{2,1,0:T(8,128)S(1)} %bitcast.4, s32[32,128]{1,0:T(8,128)S(1)} %bitcast.5, f32[6]{0:T(128)S(1)} %copy-done.4, s32[1,256]{1,0:T(1,128)S(1)} %bitcast.6, s32[1,128]{1,0:T(1,128)S(1)} %bitcast.7, f32[32,128]{1,0:T(8,128)S(1)} %copy-done.2), custom_call_target="tpu_custom_call" | custom-call | tf_op jit(solution)/shard_map/solve/pallas_call | solution.py:390
  54.4 0.7 %copy.10 = f32[3,128,128]{2,1,0:T(8,128)} copy(f32[3,128,128]{2,1,0:T(8,128)S(1)} %get-tuple-element.4) | data formatting | bytes 393216
  55.1 0.6 %copy.11 = f32[6,128]{1,0:T(8,128)} copy(f32[6,128]{1,0:T(8,128)S(1)} %get-tuple-element.5) | data formatting | bytes 6144
Async XLA Ops:
  0.6 0.7 %copy-start.5 = (s32[128]{0:T(128)S(1)}, s32[128]{0:T(128)}, u32[]{:S(2)}) copy-start(s32[128]{0:T(128)} %param.10) | copy-start | bytes 1540
  0.6 0.7 %copy-start.3 = (s32[1,1,1,256]{3,2,1,0:T(1,128)S(1)}, s32[1,1,1,256]{3,2,1,0:T(1,128)}, u32[]{:S(2)}) copy-start(s32[1,1,1,256]{3,2,1,0:T(1,128)} %param.9) | copy-start | bytes 3076
  0.7 0.7 %copy-start.4 = (f32[6]{0:T(128)S(1)}, f32[6]{0:T(128)}, u32[]{:S(2)}) copy-start(f32[6]{0:T(128)} %table.1) | copy-start | bytes 76
  1.3 1.0 %copy-start = (f32[32,4,8,128]{3,2,1,0:T(8,128)S(1)}, f32[32,4,8,128]{3,2,1,0:T(8,128)}, u32[]{:S(2)}) copy-start(f32[32,4,8,128]{3,2,1,0:T(8,128)} %param.6) | copy-start | bytes 1572868
  2.4 0.7 %copy-start.1 = (s32[4,8,128]{2,1,0:T(8,128)S(1)}, s32[4,8,128]{2,1,0:T(8,128)}, u32[]{:S(2)}) copy-start(s32[4,8,128]{2,1,0:T(8,128)} %param.7) | copy-start | bytes 49156
  3.1 0.7 %copy-start.2 = (f32[32,128]{1,0:T(8,128)S(1)}, f32[32,128]{1,0:T(8,128)}, u32[]{:S(2)}) copy-start(f32[32,128]{1,0:T(8,128)} %data.1) | copy-start | bytes 49156

commit v2 on v1

v2 whole, which is shorter than its diff:
```python
import functools

import jax
import jax.numpy as jnp
from jax import lax
from jax.experimental import pallas as pl
from jax.experimental.pallas import tpu as pltpu
from jax.sharding import PartitionSpec as P

F32 = jnp.float32
BF16 = jnp.bfloat16
MASS = 0.25
PAIRS = ((0, 0), (1, 1), (2, 2), (0, 1), (0, 2), (1, 2))
AXES = ("gx", "gy", "gz")


class Exchange:
    def __init__(self, send, recv):
        self.send, self.recv, self.used = send, recv, 0

    def start(self, source, target, axis, partner):
        return self.start_at(source, target, {axis: partner})

    def start_at(self, source, target, where):
        copy = pltpu.make_async_remote_copy(
            src_ref=source,
            dst_ref=target,
            send_sem=self.send.at[self.used],
            recv_sem=self.recv.at[self.used],
            device_id=where,
            device_id_type=pl.DeviceIdType.MESH,
        )
        self.used += 1
        copy.start()
        return copy


CHUNKS = 2


def copies_needed(sizes):
    nx, ny, nz = sizes
    plane = nx * nz - 1
    return 6 + 2 * (4 * CHUNKS + 2) + plane + 3 * (ny - 1) + 2 * (nx - 1)


def waves_needed(sizes):
    nx, ny, nz = sizes
    return max(nx // 2 - 1 + nz // 2, ny // 2 - 1)


def kernel(sizes, src, lab_in, table_in, send_in, slots_in, moments_out, owned_b_out, owned_v_out,
           lab, table, send_map, slots, field, image, xr_b, xr_v, ys_b, ys_v, yr_b, yr_v,
           zs_b, zs_v, zr_b, zr_v, zm, lys, lxr, lyr, lzr, wts, ghi, glo, onehot, pick, raw, turned,
           line_b, line_v, mid_b, mid_v, out_b, out_v, fin_b, fin_v, mq, red_plane, red_line,
           load_sem, send_sem, recv_sem, wave_sem):
    nx, ny, nz = sizes
    count = dict(zip(AXES, sizes))
    me = {axis: lax.axis_index(axis) for axis in AXES}
    low = {axis: lax.rem(me[axis] + count[axis] - 1, count[axis]) for axis in AXES}
    high = {axis: lax.rem(me[axis] + 1, count[axis]) for axis in AXES}
    has_low = {axis: me[axis] > 0 for axis in AXES}
    has_high = {axis: me[axis] < count[axis] - 1 for axis in AXES}
    keep_low = {axis: jnp.where(has_low[axis], 1.0, 0.0).astype(F32) for axis in AXES}
    keep_high = {axis: jnp.where(has_high[axis], 1.0, 0.0).astype(F32) for axis in AXES}
    sensors, cells_xy, lanes = field.shape
    cx, cy = cells_xy // 8, 8
    total_slots = send_map.shape[1]
    cap = total_slots // (nx * ny)
    per_chunk = sensors // CHUNKS
    ex = Exchange(send_sem, recv_sem)
    lane = lax.broadcasted_iota(jnp.int32, (8, lanes), 1)
    row = lax.broadcasted_iota(jnp.int32, (8, lanes), 0)

    def tell(sem, axis, partner):
        pl.semaphore_signal(
            sem, inc=1, device_id={axis: partner}, device_id_type=pl.DeviceIdType.MESH
        )

    barrier = pltpu.get_barrier_semaphore()
    for axis in AXES:
        tell(barrier, axis, low[axis])
        tell(barrier, axis, high[axis])
    loads = [pltpu.make_async_copy(lab_in, lab, load_sem.at[0])]
    for h in range(CHUNKS):
        part = pl.ds(per_chunk * h, per_chunk)
        loads.append(pltpu.make_async_copy(src.at[part], field.at[part], load_sem.at[1 + h]))
    for k, (a, b) in enumerate(((table_in, table), (send_in, send_map), (slots_in, slots))):
        loads.append(pltpu.make_async_copy(a, b, load_sem.at[1 + CHUNKS + k]))
    for copy in loads:
        copy.start()

    steps = {"gx": nx // 2 - 1, "gz": nz // 2, "gy": ny // 2 - 1}
    plan = [[] for _ in range(waves_needed(sizes))]
    for k in range(steps["gx"]):
        plan[k].append("gx")
    for k in range(steps["gz"]):
        plan[steps["gx"] + k].append("gz")
    for k in range(steps["gy"]):
        plan[k].append("gy")
    wave_at = [0]

    def wave_send():
        if wave_at[0] < len(plan):
            for axis in plan[wave_at[0]]:
                k = AXES.index(axis)
                tell(wave_sem.at[2 * k], axis, low[axis])
                tell(wave_sem.at[2 * k + 1], axis, high[axis])

    def wave(times=1):
        for _ in range(times):
            if wave_at[0] < len(plan):
                for axis in plan[wave_at[0]]:
                    k = AXES.index(axis)
                    pl.semaphore_wait(wave_sem.at[2 * k], 1)
                    pl.semaphore_wait(wave_sem.at[2 * k + 1], 1)
                wave_at[0] += 1
                wave_send()

    def x_faces(whole, xr, h):
        part = pl.ds(per_chunk * h, per_chunk)
        last = cells_xy - 8
        return [
            ex.start(whole.at[part, 0:8, :], xr.at[1, part], "gx", low["gx"]),
            ex.start(whole.at[part, last : last + 8, :], xr.at[0, part], "gx", high["gx"]),
        ]

    def y_faces(ys, yr, h):
        part = pl.ds(per_chunk * h * cx, per_chunk * cx)
        return [
            ex.start(ys.at[0, part], yr.at[1, part], "gy", low["gy"]),
            ex.start(ys.at[1, part], yr.at[0, part], "gy", high["gy"]),
        ]

    def z_faces(zs, zr):
        return [
            ex.start(zs, zr.at[1], "gz", low["gz"]),
            ex.start(zs, zr.at[0], "gz", high["gz"]),
        ]

    def pack_z(values, s, acc):
        here = lax.shift_right_logical(lane, 1) == s
        return tuple(
            jnp.where(here, pltpu.roll(values[x], 2 * s + 1, 1), acc[x]) for x in range(cx)
        )

    def store_z(zs, acc):
        for x in range(cx):
            zs[8 * x : 8 * x + 8, :] = acc[x]

    no_z = (jnp.zeros((8, lanes), F32),) * cx

    loads[0].wait()
    lys[0:cx, :] = lab[pl.ds(0, cx, stride=cy), :]
    lys[cx : 2 * cx, :] = lab[pl.ds(cy - 1, cx, stride=cy), :]
    for copy in loads[1:]:
        copy.wait()
    pl.semaphore_wait(barrier, 2 * len(AXES))
    wave_send()
    first_x = [x_faces(field, xr_b, h) for h in range(CHUNKS)]
    label_copies = [
        ex.start(lab.at[0:8, :], lxr.at[1], "gx", low["gx"]),
        ex.start(lab.at[cells_xy - 8 : cells_xy, :], lxr.at[0], "gx", high["gx"]),
        ex.start(lys, lyr.at[1], "gy", low["gy"]),
        ex.start(lys, lyr.at[0], "gy", high["gy"]),
        ex.start(lab, lzr.at[1], "gz", low["gz"]),
        ex.start(lab, lzr.at[0], "gz", high["gz"]),
    ]
    first_y = []
    for h in range(CHUNKS):
        for s in range(per_chunk * h, per_chunk * (h + 1)):
            for side, y in enumerate((0, cy - 1)):
                ys_b[side, cx * s : cx * s + cx, :] = field[s, pl.ds(y, cx, stride=cy), :]
        first_y.append(y_faces(ys_b, yr_b, h))
    store_z(
        zs_b,
        lax.fori_loop(
            0,
            sensors,
            lambda s, acc: pack_z([field[s, 8 * x : 8 * x + 8, :] for x in range(cx)], s, acc),
            no_z,
            unroll=4,
        ),
    )
    first_z = z_faces(zs_b, zr_b)

    wanted = send_map[...]
    key = lax.shift_right_arithmetic(wanted, 10) * lanes + (wanted & (lanes - 1))
    y_of = lax.shift_right_arithmetic(wanted, 7) & (cy - 1)
    for x in range(cx):
        places = lax.broadcasted_iota(jnp.int32, (lanes, total_slots), 0) + x * lanes
        onehot[x * lanes : (x + 1) * lanes, :] = jnp.where(places == key, 1.0, 0.0).astype(BF16)
    rows_in = lax.broadcasted_iota(jnp.int32, (total_slots, slots.shape[1]), 0)
    pick[...] = jnp.where(rows_in == slots[...], 1.0, 0.0).astype(BF16)
    wave(2)

    for copy in label_copies:
        copy.wait()

    def tissue(shifted):
        level = jnp.zeros(shifted.shape, F32)
        for k in range(table.shape[0]):
            level = level + jnp.where(shifted == k + 1, table[k], 0.0)
        return level, jnp.where(shifted > 0, 1.0, 0.0).astype(F32)

    shifted = [lab[8 * x : 8 * x + 8, :] + 1 for x in range(cx)]
    for x in range(cx):
        here = shifted[x]
        if x > 0:
            x_low = shifted[x - 1]
        else:
            x_low = jnp.where(has_low["gx"], lxr[0] + 1, 0)
        if x < cx - 1:
            x_high = shifted[x + 1]
        else:
            x_high = jnp.where(has_high["gx"], lxr[1] + 1, 0)
        row_low = jnp.where(has_low["gy"], lyr[0, cx + x : cx + x + 1, :] + 1, 0)
        row_high = jnp.where(has_high["gy"], lyr[1, x : x + 1, :] + 1, 0)
        y_low = jnp.where(row == 0, row_low, pltpu.roll(here, 1, 0))
        y_high = jnp.where(row == cy - 1, row_high, pltpu.roll(here, cy - 1, 0))
        side_low = jnp.where(has_low["gz"], lzr[0, 8 * x : 8 * x + 8, :] + 1, 0)
        side_high = jnp.where(has_high["gz"], lzr[1, 8 * x : 8 * x + 8, :] + 1, 0)
        z_low = pltpu.roll(jnp.where(lane == lanes - 1, side_low, here), 1, 1)
        z_high = pltpu.roll(jnp.where(lane == 0, side_high, here), lanes - 1, 1)
        own_cond, own_in = tissue(here)
        diagonal = jnp.full((8, lanes), MASS, F32)
        for k, beside in enumerate((x_low, x_high, y_low, y_high, z_low, z_high)):
            its_cond, its_in = tissue(beside)
            weight = 0.5 * (own_cond + its_cond) * own_in * its_in
            wts[k, 8 * x : 8 * x + 8, :] = weight
            diagonal = diagonal + weight
        wts[6, 8 * x : 8 * x + 8, :] = diagonal
        wts[7, 8 * x : 8 * x + 8, :] = 0.5 * own_cond
    wave()

    def merge_z(zr):
        for x in range(cx):
            span = slice(8 * x, 8 * x + 8)
            zm[span, :] = jnp.where(
                (lane & 1) == 0, zr[0, span, :] * keep_low["gz"], zr[1, span, :] * keep_high["gz"]
            )

    def neighbours(whole, xr, yr, s):
        own = [whole[s, 8 * x : 8 * x + 8, :] for x in range(cx)]
        outer = [xr[0, s] * keep_low["gx"]] + own + [xr[1, s] * keep_high["gx"]]
        near = []
        for x in range(cx):
            u = own[x]
            low_row = yr[0, pl.ds(s * cx + x, 1), :] * keep_low["gy"]
            high_row = yr[1, pl.ds(s * cx + x, 1), :] * keep_high["gy"]
            y_low = jnp.where(row == 0, low_row, pltpu.roll(u, 1, 0))
            y_high = jnp.where(row == cy - 1, high_row, pltpu.roll(u, cy - 1, 0))
            beyond = pltpu.roll(zm[8 * x : 8 * x + 8, :], lanes - 1 - 2 * s, 1)
            z_low = pltpu.roll(jnp.where(lane == lanes - 1, beyond, u), 1, 1)
            z_high = pltpu.roll(jnp.where(lane == 0, beyond, u), lanes - 1, 1)
            near.append((outer[x], outer[x + 2], y_low, y_high, z_low, z_high))
        return own, near

    def apply(own, near, x):
        span = slice(8 * x, 8 * x + 8)
        q = wts[6, span, :] * own[x]
        for n in range(6):
            q = q - wts[n, span, :] * near[x][n]
        return q

    def rows_of(s):
        return pl.ds(pl.multiple_of(8 * s, 8), 8)

    def image_pass(i, acc):
        for k in range(2):
            s = 2 * i + k
            own, near = neighbours(field, xr_b, yr_b, s)
            results = [apply(own, near, x) for x in range(cx)]
            for x in range(cx):
                image[s, 8 * x : 8 * x + 8, :] = results[x]
                ys_v[0, pl.ds(s * cx + x, 1), :] = results[x][0:1, :]
                ys_v[1, pl.ds(s * cx + x, 1), :] = results[x][cy - 1 : cy, :]
            acc = pack_z(results, s, acc)
        return acc

    def energy_pass(i, carry):
        for k in range(2):
            s = 2 * i + k
            own, near = neighbours(image, xr_v, yr_v, s)
            term = own[0] * apply(own, near, 0)
            for x in range(1, cx):
                term = term + own[x] * apply(own, near, x)
            mq[3, rows_of(s), :] = term
        return carry

    def slope_pass(whole, xr, yr, result, i):
        slopes = [[[None, None] for _ in range(cx)] for _ in range(3)]
        for k in range(2):
            s = 2 * i + k
            own, near = neighbours(whole, xr, yr, s)
            sums = [None, None, None]
            for x in range(cx):
                half = wts[7, 8 * x : 8 * x + 8, :]
                for c in range(3):
                    slopes[c][x][k] = half * (near[x][2 * c + 1] - near[x][2 * c])
                if result is not None:
                    q = result[s, 8 * x : 8 * x + 8, :]
                    for n, term in enumerate((own[x] * own[x], own[x] * q, q * q)):
                        sums[n] = term if sums[n] is None else sums[n] + term
            if result is not None:
                for n in range(3):
                    mq[n, rows_of(s), :] = sums[n]
        at = pl.ds(pl.multiple_of(16 * i, 16), 16)
        for c in range(3):
            for x in range(cx):
                slope = jnp.concatenate(slopes[c][x], axis=0)
                coarse = slope.astype(BF16)
                ghi[c, at, x * lanes : (x + 1) * lanes] = coarse
                glo[c, at, x * lanes : (x + 1) * lanes] = (slope - coarse.astype(F32)).astype(BF16)

    def slopes_of(whole, xr, yr, result):
        def step(i, carry):
            slope_pass(whole, xr, yr, result, i)
            return carry

        lax.fori_loop(0, sensors // 2, step, 0)

    def gather(line):
        parts = []
        for c in range(3):
            product = jnp.dot(ghi[c], onehot[...], preferred_element_type=F32) + jnp.dot(
                glo[c], onehot[...], preferred_element_type=F32
            )
            for h in range(total_slots // lanes):
                raw[h] = product[:, h * lanes : (h + 1) * lanes]
            for g in range(sensors // 8):
                halves = []
                for h in range(total_slots // lanes):
                    acc = None
                    for y in range(cy):
                        strip = raw[h, pl.ds(8 * cy * g + y, 8, stride=cy), :]
                        term = jnp.where(y_of[:, h * lanes : (h + 1) * lanes] == y, strip, 0.0)
                        acc = term if acc is None else acc + term
                    halves.append(acc)
                parts.append(jnp.concatenate(halves, axis=1))
        parts.append(jnp.zeros((lanes - 3 * sensors, total_slots), F32))
        turned[...] = jnp.concatenate(parts, axis=0).T
        for j in range(ny * cap):
            line[j * nx : (j + 1) * nx, :] = turned[pl.ds(j, nx, stride=ny * cap), :]

    def spread(source, target, axis):
        rows = source.shape[0] // count[axis]
        mine = pl.ds(pl.multiple_of(me[axis] * rows, rows), rows)
        copies = []
        for d in range(1, count[axis]):
            partner = lax.rem(me[axis] + d, count[axis])
            theirs = pl.ds(pl.multiple_of(partner * rows, rows), rows)
            copies.append(ex.start(source.at[theirs, :], target.at[mine, :], axis, partner))
        target[mine, :] = source[mine, :]
        return copies

    def regroup(mid, out):
        rows = ny * cap
        for ix in range(nx):
            out[ix * rows : (ix + 1) * rows, :] = mid[pl.ds(ix, rows, stride=nx), :]

    def reduce_start(buffer, value, partners):
        buffer[0] = value
        return [
            ex.start_at(buffer.at[0], buffer.at[k + 1], where) for k, where in enumerate(partners)
        ]

    def reduce_end(buffer, copies):
        for copy in copies:
            copy.wait()
        value = buffer[0]
        for d in range(1, len(copies) + 1):
            value = value + buffer[d]
        return value

    def moment_rows(m):
        parts = []
        for g in range(sensors // 8):
            acc = None
            for y in range(cy):
                strip = mq[m, pl.ds(8 * cy * g + y, 8, stride=cy), :]
                acc = strip if acc is None else acc + strip
            parts.append(acc)
        return parts

    def lane_sums(parts):
        return lax.dot_general(
            jnp.ones((8, lanes), F32),
            jnp.concatenate(parts, axis=0),
            (((1,), (1,)), ((), ())),
            precision=lax.Precision.HIGHEST,
            preferred_element_type=F32,
        )[0:1, :]

    def select(fin):
        columns = fin[...].T
        coarse = columns.astype(BF16)
        fine = (columns - coarse.astype(F32)).astype(BF16)
        return jnp.dot(coarse, pick[...], preferred_element_type=F32) + jnp.dot(
            fine, pick[...], preferred_element_type=F32
        )

    def wait(copies):
        for copy in copies:
            copy.wait()

    blank = [jnp.zeros((8, lanes), F32)]
    half_pairs = per_chunk // 2
    wait(first_z)
    merge_z(zr_b)
    acc = no_z
    second = []
    for h in range(CHUNKS):
        wait(first_x[h] + first_y[h])
        acc = lax.fori_loop(half_pairs * h, half_pairs * (h + 1), image_pass, acc)
        second.append(x_faces(image, xr_v, h) + y_faces(ys_v, yr_v, h))
    store_z(zs_v, acc)
    second_z = z_faces(zs_v, zr_v)
    wave()
    slopes_of(field, xr_b, yr_b, image)
    wave()
    early = lane_sums(moment_rows(0) + moment_rows(1) + moment_rows(2) + blank * (sensors // 8))
    gather(line_b)
    wave(len(plan))
    line_b_copies = spread(line_b, mid_b, "gy")
    wait(second_z)
    merge_z(zr_v)
    for h in range(CHUNKS):
        wait(second[h])
        lax.fori_loop(half_pairs * h, half_pairs * (h + 1), energy_pass, 0)
    partial = early + lane_sums(blank * (3 * sensors // 8) + moment_rows(3))
    plane = [
        {"gx": lax.rem(me["gx"] + dx, nx), "gz": lax.rem(me["gz"] + dz, nz)}
        for dx in range(nx)
        for dz in range(nz)
        if dx or dz
    ]
    plane_copies = reduce_start(red_plane, partial, plane)
    slopes_of(image, xr_v, yr_v, None)
    gather(line_v)
    line_v_copies = spread(line_v, mid_v, "gy")
    line = [{"gy": lax.rem(me["gy"] + d, ny)} for d in range(1, ny)]
    line_copies = reduce_start(red_line, reduce_end(red_plane, plane_copies), line)
    wait(line_b_copies)
    regroup(mid_b, out_b)
    out_b_copies = spread(out_b, fin_b, "gx")
    wait(line_v_copies)
    regroup(mid_v, out_v)
    out_v_copies = spread(out_v, fin_v, "gx")
    wait(out_b_copies)
    owned_b_out[...] = select(fin_b)
    wait(out_v_copies)
    owned_v_out[...] = select(fin_v)
    moments_out[...] = jnp.broadcast_to(reduce_end(red_line, line_copies), (8, lanes))


def finish(moments_in, owned_b, owned_v, data, proj, gram):
    sensors = data.shape[0]
    moments = moments_in[...]
    lanes = moments.shape[1]
    group = lax.broadcasted_iota(jnp.int32, moments.shape, 1) // sensors
    full = []
    for m in range(4):
        value = moments
        for g in range(lanes // sensors):
            shift = (sensors * (g - m)) % lanes
            turn = pltpu.roll(moments, shift, 1) if shift else moments
            value = jnp.where(group == g, turn, value)
        full.append(value)
    zero, one, two, three = full
    first_step = zero / one
    residue = first_step * first_step * two - zero
    growth = 1.0 + residue / zero
    curvature = growth * growth * one - 2.0 * growth * first_step * two + first_step * first_step * three
    second_step = residue / curvature
    source_coef = (first_step + second_step * growth)[0:1, :]
    image_coef = (second_step * first_step)[0:1, :]
    down = (lanes, lanes)
    owned = jnp.broadcast_to(source_coef, down).T * owned_b[...] - jnp.broadcast_to(image_coef, down).T * owned_v[...]
    per_time = data[...].T
    parts = [owned[sensors * c : sensors * (c + 1), :] for c in range(3)]
    for c in range(3):
        proj[c] = jnp.dot(
            per_time, parts[c], precision=lax.Precision.HIGHEST, preferred_element_type=F32
        )
    for k, (a, b) in enumerate(PAIRS):
        gram[k : k + 1, :] = jnp.sum(parts[a] * parts[b], axis=0, keepdims=True)


def per_device(sizes, source_term, labels, table, send_map, owner_slots, sensor_data):
    sensors, cx, cy, lanes = source_term.shape
    cells_xy = cx * cy
    total = send_map.shape[-1]
    owned = owner_slots.shape[0]
    times = sensor_data.shape[1]
    n = copies_needed(sizes)
    vmem = pltpu.VMEM
    scratch = [
        vmem((cells_xy, lanes), jnp.int32),
        pltpu.SMEM(table.shape, F32),
        vmem((1, total), jnp.int32),
        vmem((1, owned), jnp.int32),
        vmem((sensors, cells_xy, lanes), F32),
        vmem((sensors, cells_xy, lanes), F32),
        vmem((2, sensors, 8, lanes), F32),
        vmem((2, sensors, 8, lanes), F32),
        vmem((2, sensors * cx, lanes), F32),
        vmem((2, sensors * cx, lanes), F32),
        vmem((2, sensors * cx, lanes), F32),
        vmem((2, sensors * cx, lanes), F32),
        vmem((cells_xy, lanes), F32),
        vmem((cells_xy, lanes), F32),
        vmem((2, cells_xy, lanes), F32),
        vmem((2, cells_xy, lanes), F32),
        vmem((cells_xy, lanes), F32),
        vmem((2 * cx, lanes), jnp.int32),
        vmem((2, 8, lanes), jnp.int32),
        vmem((2, 2 * cx, lanes), jnp.int32),
        vmem((2, cells_xy, lanes), jnp.int32),
        vmem((8, cells_xy, lanes), F32),
        vmem((3, sensors * 8, cx * lanes), BF16),
        vmem((3, sensors * 8, cx * lanes), BF16),
        vmem((cx * lanes, total), BF16),
        vmem((total, owned), BF16),
        vmem((total // lanes, sensors * 8, lanes), F32),
        vmem((total, lanes), F32),
    ]
    scratch += [vmem((total, lanes), F32)] * 8
    scratch += [
        vmem((4, sensors * 8, lanes), F32),
        vmem((sizes[0] * sizes[2], 1, lanes), F32),
        vmem((sizes[1], 1, lanes), F32),
        pltpu.SemaphoreType.DMA((4 + CHUNKS,)),
        pltpu.SemaphoreType.DMA((n,)),
        pltpu.SemaphoreType.DMA((n,)),
        pltpu.SemaphoreType.REGULAR((2 * len(AXES),)),
    ]
    whole = pl.BlockSpec(memory_space=pltpu.VMEM)
    moments, owned_b, owned_v = pl.pallas_call(
        functools.partial(kernel, sizes),
        out_shape=(
            jax.ShapeDtypeStruct((8, lanes), F32),
            jax.ShapeDtypeStruct((lanes, owned), F32),
            jax.ShapeDtypeStruct((lanes, owned), F32),
        ),
        in_specs=[pl.BlockSpec(memory_space=pltpu.HBM)] * 5,
        out_specs=(whole,) * 3,
        scratch_shapes=scratch,
        compiler_params=pltpu.CompilerParams(
            collective_id=0, has_side_effects=True, vmem_limit_bytes=40 * 1024 * 1024
        ),
        name="solve",
    )(
        *(
            pltpu.with_memory_space_constraint(operand, pltpu.HBM)
            for operand in (
                source_term.reshape(sensors, cells_xy, lanes),
                labels.reshape(cells_xy, lanes),
                table,
                send_map.reshape(1, total),
                owner_slots.reshape(1, owned),
            )
        )
    )
    return pl.pallas_call(
        finish,
        out_shape=(
            jax.ShapeDtypeStruct((3, times, owned), F32),
            jax.ShapeDtypeStruct((len(PAIRS), owned), F32),
        ),
        in_specs=[whole] * 4,
        out_specs=(whole, whole),
        compiler_params=pltpu.CompilerParams(vmem_limit_bytes=40 * 1024 * 1024),
        name="finish",
    )(moments, owned_b, owned_v, sensor_data)


def solution(mesh):
    sizes = tuple(mesh.shape[axis] for axis in AXES)
    in_specs = (
        P(None, "gx", "gy", "gz"),
        P("gx", "gy", "gz"),
        P(),
        P("gx", "gy", "gz", None),
        P(AXES),
        P(),
    )
    out_specs = (P(None, None, AXES), P(None, AXES))
    return jax.shard_map(
        functools.partial(per_device, sizes),
        mesh=mesh,
        in_specs=in_specs,
        out_specs=out_specs,
        check_vma=False,
    )
```

time: 56 us -> 52.8 us (0.943)
  local copies, waits for them, and re-layouts: 4.42 us -> 0.01 us
  Pallas kernels: 50.6 us -> 52 us
    unnamed x14 -> x2, local copies, waits for them, and re-layouts: 4.42 us -> 0.01 us
    pallas_call x0 -> x1, Pallas kernels: none -> 1.17 us  [per_device(): pl.pallas_call(finish, out_shape=(jax.ShapeDtypeStruct((3, times, owned),...]
where the time goes in v2:
time: 52.8 us; the launch traced here: 52.7 us
  Pallas kernels  52 us (98%)
  between operations  0.66 us (1%)
    pallas_call x1, Pallas kernels, per_device(): pl.pallas_call(functools.partial(kernel, sizes), out_shape=(jax.ShapeDtyp...  50.8 us
    pallas_call x1, Pallas kernels, per_device(): pl.pallas_call(finish, out_shape=(jax.ShapeDtypeStruct((3, times, owned),...  1.17 us

profile of v2, /device:TPU:1, one launch (start us, length us, event | category | flops | bytes accessed | tf_op | source)
XLA Modules:
  0.0 52.7 jit_solution(799857874895554306)
XLA Ops:
  0.6 0.0 copy-start
  0.6 50.8 %solve.1 = (f32[8,128]{1,0:T(8,128)S(1)}, f32[128,128]{1,0:T(8,128)S(1)}, f32[128,128]{1,0:T(8,128)S(1)}) custom-call(f32[32,32,128]{2,1,0:T(8,128)} %bitcast.4, s32[32,128]{1,0:T(8,128)} %bitcast.5, f32[6]{0:T(128)} %table_in.1, s32[1,256]{1,0:T(1,128)} %bitcast.6, s32[1,128]{1,0:T(1,128)} %bitcast.7), custom_call_target="tpu_custom_call" | custom-call | tf_op jit(solution)/shard_map/solve/pallas_call | solution.py:539
  51.5 0.0 copy-done
  51.5 1.2 %finish.1 = (f32[3,128,128]{2,1,0:T(8,128)}, f32[6,128]{1,0:T(8,128)}) custom-call(f32[8,128]{1,0:T(8,128)S(1)} %get-tuple-element.5.moments_in, f32[128,128]{1,0:T(8,128)S(1)} %get-tuple-element.6.owned_b, f32[128,128]{1,0:T(8,128)S(1)} %get-tuple-element.7.owned_v, f32[32,128]{1,0:T(8,128)S(1)} %copy-done), custom_call_target="tpu_custom_call" | custom-call | tf_op jit(solution)/shard_map/finish/pallas_call | solution.py:565
Async XLA Ops:
  0.6 50.8 %copy-start = (f32[32,128]{1,0:T(8,128)S(1)}, f32[32,128]{1,0:T(8,128)}, u32[]{:S(2)}) copy-start(f32[32,128]{1,0:T(8,128)} %data.1) | copy-start | bytes 49156

commit v3 on v2

--- a/solution.py
+++ b/solution.py
@@ -36,6 +36,7 @@
 
 
 CHUNKS = 2
+UNROLL = 8
 
 
 def copies_needed(sizes):
@@ -44,14 +45,28 @@
     return 6 + 2 * (4 * CHUNKS + 2) + plane + 3 * (ny - 1) + 2 * (nx - 1)
 
 
-def waves_needed(sizes):
+def doubling(known, size):
+    strides = []
+    while known < size // 2:
+        strides.append(max(known, 1))
+        known += strides[-1]
+    return strides
+
+
+def wave_plan(sizes):
     nx, ny, nz = sizes
-    return max(nx // 2 - 1 + nz // 2, ny // 2 - 1)
+    across = [("gx", d) for d in doubling(1, nx)] + [("gz", d) for d in doubling(0, nz)]
+    along = [("gy", d) for d in doubling(1, ny)]
+    plan = [[] for _ in range(max(len(across), len(along)))]
+    for steps in (across, along):
+        for k, step in enumerate(steps):
+            plan[k].append(step)
+    return plan
 
 
 def kernel(sizes, src, lab_in, table_in, send_in, slots_in, moments_out, owned_b_out, owned_v_out,
            lab, table, send_map, slots, field, image, xr_b, xr_v, ys_b, ys_v, yr_b, yr_v,
-           zs_b, zs_v, zr_b, zr_v, zm, lys, lxr, lyr, lzr, wts, ghi, glo, onehot, pick, raw, turned,
+           zs_b, zs_v, zr_b, zr_v, zm, lys, lxr, lyr, lzr, wts, ghi, glo, onehot, pick, raw,
            line_b, line_v, mid_b, mid_v, out_b, out_v, fin_b, fin_v, mq, red_plane, red_line,
            load_sem, send_sem, recv_sem, wave_sem):
     nx, ny, nz = sizes
@@ -90,30 +105,28 @@
     for copy in loads:
         copy.start()
 
-    steps = {"gx": nx // 2 - 1, "gz": nz // 2, "gy": ny // 2 - 1}
-    plan = [[] for _ in range(waves_needed(sizes))]
-    for k in range(steps["gx"]):
-        plan[k].append("gx")
-    for k in range(steps["gz"]):
-        plan[steps["gx"] + k].append("gz")
-    for k in range(steps["gy"]):
-        plan[k].append("gy")
+    plan = wave_plan(sizes)
     wave_at = [0]
 
+    def wave_sems(k, axis):
+        first = 2 * (len(AXES) * k + AXES.index(axis))
+        return wave_sem.at[first], wave_sem.at[first + 1]
+
     def wave_send():
-        if wave_at[0] < len(plan):
-            for axis in plan[wave_at[0]]:
-                k = AXES.index(axis)
-                tell(wave_sem.at[2 * k], axis, low[axis])
-                tell(wave_sem.at[2 * k + 1], axis, high[axis])
+        k = wave_at[0]
+        if k < len(plan):
+            for axis, stride in plan[k]:
+                down, up = wave_sems(k, axis)
+                tell(down, axis, lax.rem(me[axis] + count[axis] - stride, count[axis]))
+                tell(up, axis, lax.rem(me[axis] + stride, count[axis]))
 
     def wave(times=1):
         for _ in range(times):
-            if wave_at[0] < len(plan):
-                for axis in plan[wave_at[0]]:
-                    k = AXES.index(axis)
-                    pl.semaphore_wait(wave_sem.at[2 * k], 1)
-                    pl.semaphore_wait(wave_sem.at[2 * k + 1], 1)
+            k = wave_at[0]
+            if k < len(plan):
+                for axis, _stride in plan[k]:
+                    for sem in wave_sems(k, axis):
+                        pl.semaphore_wait(sem, 1)
                 wave_at[0] += 1
                 wave_send()
 
@@ -179,7 +192,7 @@
             sensors,
             lambda s, acc: pack_z([field[s, 8 * x : 8 * x + 8, :] for x in range(cx)], s, acc),
             no_z,
-            unroll=4,
+            unroll=16,
         ),
     )
     first_z = z_faces(zs_b, zr_b)
@@ -191,8 +204,10 @@
         places = lax.broadcasted_iota(jnp.int32, (lanes, total_slots), 0) + x * lanes
         onehot[x * lanes : (x + 1) * lanes, :] = jnp.where(places == key, 1.0, 0.0).astype(BF16)
     rows_in = lax.broadcasted_iota(jnp.int32, (total_slots, slots.shape[1]), 0)
-    pick[...] = jnp.where(rows_in == slots[...], 1.0, 0.0).astype(BF16)
-    wave(2)
+    slot_cap, slot_y = slots[...] % cap, slots[...] // cap % ny
+    slot_row = slot_y * (nx * cap) + slot_cap * nx + slots[...] // (cap * ny)
+    pick[...] = jnp.where(rows_in == slot_row, 1.0, 0.0).astype(BF16)
+    wave()
 
     for copy in label_copies:
         copy.wait()
@@ -237,22 +252,28 @@
         for x in range(cx):
             span = slice(8 * x, 8 * x + 8)
             zm[span, :] = jnp.where(
-                (lane & 1) == 0, zr[0, span, :] * keep_low["gz"], zr[1, span, :] * keep_high["gz"]
+                (lane & 1) == 0,
+                pltpu.roll(zr[0, span, :], 2, 1) * keep_low["gz"],
+                zr[1, span, :] * keep_high["gz"],
             )
 
-    def neighbours(whole, xr, yr, s):
+    def neighbours(whole, xr, yr, s, masked):
         own = [whole[s, 8 * x : 8 * x + 8, :] for x in range(cx)]
-        outer = [xr[0, s] * keep_low["gx"]] + own + [xr[1, s] * keep_high["gx"]]
+        outer = [xr[0, s]] + own + [xr[1, s]]
+        if masked:
+            outer[0], outer[-1] = outer[0] * keep_low["gx"], outer[-1] * keep_high["gx"]
         near = []
         for x in range(cx):
             u = own[x]
-            low_row = yr[0, pl.ds(s * cx + x, 1), :] * keep_low["gy"]
-            high_row = yr[1, pl.ds(s * cx + x, 1), :] * keep_high["gy"]
+            low_row = yr[0, pl.ds(s * cx + x, 1), :]
+            high_row = yr[1, pl.ds(s * cx + x, 1), :]
+            if masked:
+                low_row, high_row = low_row * keep_low["gy"], high_row * keep_high["gy"]
             y_low = jnp.where(row == 0, low_row, pltpu.roll(u, 1, 0))
             y_high = jnp.where(row == cy - 1, high_row, pltpu.roll(u, cy - 1, 0))
-            beyond = pltpu.roll(zm[8 * x : 8 * x + 8, :], lanes - 1 - 2 * s, 1)
-            z_low = pltpu.roll(jnp.where(lane == lanes - 1, beyond, u), 1, 1)
-            z_high = pltpu.roll(jnp.where(lane == 0, beyond, u), lanes - 1, 1)
+            beyond = pltpu.roll(zm[8 * x : 8 * x + 8, :], lanes - 2 - 2 * s, 1)
+            z_low = jnp.where(lane == 0, beyond, pltpu.roll(u, 1, 1))
+            z_high = jnp.where(lane == lanes - 1, beyond, pltpu.roll(u, lanes - 1, 1))
             near.append((outer[x], outer[x + 2], y_low, y_high, z_low, z_high))
         return own, near
 
@@ -267,9 +288,9 @@
         return pl.ds(pl.multiple_of(8 * s, 8), 8)
 
     def image_pass(i, acc):
-        for k in range(2):
-            s = 2 * i + k
-            own, near = neighbours(field, xr_b, yr_b, s)
+        for k in range(UNROLL):
+            s = UNROLL * i + k
+            own, near = neighbours(field, xr_b, yr_b, s, False)
             results = [apply(own, near, x) for x in range(cx)]
             for x in range(cx):
                 image[s, 8 * x : 8 * x + 8, :] = results[x]
@@ -279,9 +300,9 @@
         return acc
 
     def energy_pass(i, carry):
-        for k in range(2):
-            s = 2 * i + k
-            own, near = neighbours(image, xr_v, yr_v, s)
+        for k in range(UNROLL):
+            s = UNROLL * i + k
+            own, near = neighbours(image, xr_v, yr_v, s, False)
             term = own[0] * apply(own, near, 0)
             for x in range(1, cx):
                 term = term + own[x] * apply(own, near, x)
@@ -292,7 +313,7 @@
         slopes = [[[None, None] for _ in range(cx)] for _ in range(3)]
         for k in range(2):
             s = 2 * i + k
-            own, near = neighbours(whole, xr, yr, s)
+            own, near = neighbours(whole, xr, yr, s, True)
             sums = [None, None, None]
             for x in range(cx):
                 half = wts[7, 8 * x : 8 * x + 8, :]
@@ -315,10 +336,11 @@
 
     def slopes_of(whole, xr, yr, result):
         def step(i, carry):
-            slope_pass(whole, xr, yr, result, i)
+            for k in range(UNROLL // 2):
+                slope_pass(whole, xr, yr, result, UNROLL // 2 * i + k)
             return carry
 
-        lax.fori_loop(0, sensors // 2, step, 0)
+        lax.fori_loop(0, sensors // UNROLL, step, 0)
 
     def gather(line):
         parts = []
@@ -339,9 +361,7 @@
                     halves.append(acc)
                 parts.append(jnp.concatenate(halves, axis=1))
         parts.append(jnp.zeros((lanes - 3 * sensors, total_slots), F32))
-        turned[...] = jnp.concatenate(parts, axis=0).T
-        for j in range(ny * cap):
-            line[j * nx : (j + 1) * nx, :] = turned[pl.ds(j, nx, stride=ny * cap), :]
+        line[...] = jnp.concatenate(parts, axis=0).T
 
     def spread(source, target, axis):
         rows = source.shape[0] // count[axis]
@@ -354,10 +374,44 @@
         target[mine, :] = source[mine, :]
         return copies
 
+    def spread_slabs(source, target, axis):
+        mine = me[axis]
+        copies = []
+        for d in range(1, count[axis]):
+            partner = lax.rem(mine + d, count[axis])
+            copies.append(ex.start(source.at[partner], target.at[mine], axis, partner))
+        target[mine] = source[mine]
+        return copies
+
+    tail = lane >= 3 * sensors
+    first_rows = row < 4
+
     def regroup(mid, out):
-        rows = ny * cap
-        for ix in range(nx):
-            out[ix * rows : (ix + 1) * rows, :] = mid[pl.ds(ix, rows, stride=nx), :]
+        for iy in range(ny):
+            rows = jnp.concatenate(
+                [mid[pl.ds(iy * cap + t, nx, stride=ny * cap), :] for t in range(cap)], axis=0
+            )
+            for g in range(nx * cap // 16):
+                a, b = rows[16 * g : 16 * g + 8, :], rows[16 * g + 8 : 16 * g + 16, :]
+                p0 = pltpu.roll(pltpu.roll(b, lanes - sensors, 1), 4, 0)
+                p1 = pltpu.roll(b, lanes - 2 * sensors, 1)
+                p2 = pltpu.roll(pltpu.roll(b, lanes - 3 * sensors, 1), 4, 0)
+                out[iy, 12 * g : 12 * g + 8, :] = jnp.where(tail, jnp.where(first_rows, p0, p1), a)
+                out[iy, 12 * g + 8 : 12 * g + 12, :] = jnp.where(tail, p2, b)[0:4, :]
+
+    def unpack(slabs):
+        parts = []
+        third = lane // sensors
+        for iy in range(ny):
+            for g in range(nx * cap // 16):
+                a = slabs[iy, 12 * g : 12 * g + 8, :]
+                b = jnp.concatenate([slabs[iy, 12 * g + 8 : 12 * g + 12, :]] * 2, axis=0)
+                p0 = pltpu.roll(pltpu.roll(a, sensors, 1), 4, 0)
+                p1 = pltpu.roll(a, 2 * sensors, 1)
+                p2 = pltpu.roll(b, 3 * sensors, 1)
+                last = jnp.where(third == 0, p0, jnp.where(third == 1, p1, p2))
+                parts += [a, jnp.where(first_rows, b, last)]
+        return jnp.concatenate(parts, axis=0)
 
     def reduce_start(buffer, value, partners):
         buffer[0] = value
@@ -393,7 +447,7 @@
         )[0:1, :]
 
     def select(fin):
-        columns = fin[...].T
+        columns = unpack(fin).T
         coarse = columns.astype(BF16)
         fine = (columns - coarse.astype(F32)).astype(BF16)
         return jnp.dot(coarse, pick[...], preferred_element_type=F32) + jnp.dot(
@@ -405,30 +459,29 @@
             copy.wait()
 
     blank = [jnp.zeros((8, lanes), F32)]
-    half_pairs = per_chunk // 2
+    steps_per_chunk = per_chunk // UNROLL
     wait(first_z)
     merge_z(zr_b)
     acc = no_z
     second = []
     for h in range(CHUNKS):
         wait(first_x[h] + first_y[h])
-        acc = lax.fori_loop(half_pairs * h, half_pairs * (h + 1), image_pass, acc)
+        acc = lax.fori_loop(steps_per_chunk * h, steps_per_chunk * (h + 1), image_pass, acc)
         second.append(x_faces(image, xr_v, h) + y_faces(ys_v, yr_v, h))
     store_z(zs_v, acc)
     second_z = z_faces(zs_v, zr_v)
     wave()
     slopes_of(field, xr_b, yr_b, image)
-    wave()
     early = lane_sums(moment_rows(0) + moment_rows(1) + moment_rows(2) + blank * (sensors // 8))
     gather(line_b)
-    wave(len(plan))
-    line_b_copies = spread(line_b, mid_b, "gy")
+    line_b_copies = spread(line_b, mid_b, "gx")
     wait(second_z)
     merge_z(zr_v)
     for h in range(CHUNKS):
         wait(second[h])
-        lax.fori_loop(half_pairs * h, half_pairs * (h + 1), energy_pass, 0)
+        lax.fori_loop(steps_per_chunk * h, steps_per_chunk * (h + 1), energy_pass, 0)
     partial = early + lane_sums(blank * (3 * sensors // 8) + moment_rows(3))
+    wave(len(plan))
     plane = [
         {"gx": lax.rem(me["gx"] + dx, nx), "gz": lax.rem(me["gz"] + dz, nz)}
         for dx in range(nx)
@@ -436,17 +489,17 @@
         if dx or dz
     ]
     plane_copies = reduce_start(red_plane, partial, plane)
+    wait(line_b_copies)
+    regroup(mid_b, out_b)
+    out_b_copies = spread_slabs(out_b, fin_b, "gy")
     slopes_of(image, xr_v, yr_v, None)
     gather(line_v)
-    line_v_copies = spread(line_v, mid_v, "gy")
+    line_v_copies = spread(line_v, mid_v, "gx")
     line = [{"gy": lax.rem(me["gy"] + d, ny)} for d in range(1, ny)]
     line_copies = reduce_start(red_line, reduce_end(red_plane, plane_copies), line)
-    wait(line_b_copies)
-    regroup(mid_b, out_b)
-    out_b_copies = spread(out_b, fin_b, "gx")
     wait(line_v_copies)
     regroup(mid_v, out_v)
-    out_v_copies = spread(out_v, fin_v, "gx")
+    out_v_copies = spread_slabs(out_v, fin_v, "gy")
     wait(out_b_copies)
     owned_b_out[...] = select(fin_b)
     wait(out_v_copies)
@@ -523,9 +576,10 @@
         vmem((cx * lanes, total), BF16),
         vmem((total, owned), BF16),
         vmem((total // lanes, sensors * 8, lanes), F32),
-        vmem((total, lanes), F32),
     ]
-    scratch += [vmem((total, lanes), F32)] * 8
+    slabs = (sizes[1], total // sizes[1] * 3 // 4, lanes)
+    scratch += [vmem((total, lanes), F32)] * 4
+    scratch += [vmem(slabs, F32)] * 4
     scratch += [
         vmem((4, sensors * 8, lanes), F32),
         vmem((sizes[0] * sizes[2], 1, lanes), F32),
@@ -533,7 +587,7 @@
         pltpu.SemaphoreType.DMA((4 + CHUNKS,)),
         pltpu.SemaphoreType.DMA((n,)),
         pltpu.SemaphoreType.DMA((n,)),
-        pltpu.SemaphoreType.REGULAR((2 * len(AXES),)),
+        pltpu.SemaphoreType.REGULAR((2 * len(AXES) * len(wave_plan(sizes)),)),
     ]
     whole = pl.BlockSpec(memory_space=pltpu.VMEM)
     moments, owned_b, owned_v = pl.pallas_call(

time: 52.8 us -> 44.6 us (0.84)
  Pallas kernels: 52 us -> 43.7 us
    pallas_call x1, Pallas kernels: 50.8 us -> 42.5 us  [per_device(): pl.pallas_call(functools.partial(kernel, sizes), out_shape=(jax.ShapeDtyp...]
where the time goes in v3:
time: 44.6 us; the launch traced here: 44.4 us
  Pallas kernels  43.7 us (98%)
  between operations  0.66 us (1%)
    pallas_call x1, Pallas kernels, per_device(): pl.pallas_call(functools.partial(kernel, sizes), out_shape=(jax.ShapeDtyp...  42.5 us
    pallas_call x1, Pallas kernels, per_device(): pl.pallas_call(finish, out_shape=(jax.ShapeDtypeStruct((3, times, owned),...  1.17 us

profile of v3, /device:TPU:1, one launch (start us, length us, event | category | flops | bytes accessed | tf_op | source)
XLA Modules:
  0.0 44.4 jit_solution(5949739540753625708)
XLA Ops:
  0.6 0.0 copy-start
  0.6 42.5 %solve.1 = (f32[8,128]{1,0:T(8,128)S(1)}, f32[128,128]{1,0:T(8,128)S(1)}, f32[128,128]{1,0:T(8,128)S(1)}) custom-call(f32[32,32,128]{2,1,0:T(8,128)} %bitcast.4, s32[32,128]{1,0:T(8,128)} %bitcast.5, f32[6]{0:T(128)} %table_in.1, s32[1,256]{1,0:T(1,128)} %bitcast.6, s32[1,128]{1,0:T(1,128)} %bitcast.7), custom_call_target="tpu_custom_call" | custom-call | tf_op jit(solution)/shard_map/solve/pallas_call | solution.py:593
  43.2 0.0 copy-done
  43.2 1.2 %finish.1 = (f32[3,128,128]{2,1,0:T(8,128)}, f32[6,128]{1,0:T(8,128)}) custom-call(f32[8,128]{1,0:T(8,128)S(1)} %get-tuple-element.5.moments_in, f32[128,128]{1,0:T(8,128)S(1)} %get-tuple-element.6.owned_b, f32[128,128]{1,0:T(8,128)S(1)} %get-tuple-element.7.owned_v, f32[32,128]{1,0:T(8,128)S(1)} %copy-done), custom_call_target="tpu_custom_call" | custom-call | tf_op jit(solution)/shard_map/finish/pallas_call | solution.py:619
Async XLA Ops:
  0.6 42.6 %copy-start = (f32[32,128]{1,0:T(8,128)S(1)}, f32[32,128]{1,0:T(8,128)}, u32[]{:S(2)}) copy-start(f32[32,128]{1,0:T(8,128)} %data.1) | copy-start | bytes 49156

commit v4 on v3

--- a/solution.py
+++ b/solution.py
@@ -45,6 +45,10 @@
     return 6 + 2 * (4 * CHUNKS + 2) + plane + 3 * (ny - 1) + 2 * (nx - 1)
 
 
+def farthest_first(size):
+    return sorted(range(1, size), key=lambda d: -min(d, size - d))
+
+
 def doubling(known, size):
     strides = []
     while known < size // 2:
@@ -66,8 +70,8 @@
 
 def kernel(sizes, src, lab_in, table_in, send_in, slots_in, moments_out, owned_b_out, owned_v_out,
            lab, table, send_map, slots, field, image, xr_b, xr_v, ys_b, ys_v, yr_b, yr_v,
-           zs_b, zs_v, zr_b, zr_v, zm, lys, lxr, lyr, lzr, wts, ghi, glo, onehot, pick, raw,
-           line_b, line_v, mid_b, mid_v, out_b, out_v, fin_b, fin_v, mq, red_plane, red_line,
+           zs_b, zs_v, zr_b, zr_v, zm, lys, lxr, lyr, lzr, wts, ghi, glo, onehot, pick_b, pick_v, raw,
+           line_b, line_v, mid_b, mid_v, turn_b, last_b, out_b, out_v, fin_b, fin_v, mq, red_plane, red_line,
            load_sem, send_sem, recv_sem, wave_sem):
     nx, ny, nz = sizes
     count = dict(zip(AXES, sizes))
@@ -92,10 +96,6 @@
             sem, inc=1, device_id={axis: partner}, device_id_type=pl.DeviceIdType.MESH
         )
 
-    barrier = pltpu.get_barrier_semaphore()
-    for axis in AXES:
-        tell(barrier, axis, low[axis])
-        tell(barrier, axis, high[axis])
     loads = [pltpu.make_async_copy(lab_in, lab, load_sem.at[0])]
     for h in range(CHUNKS):
         part = pl.ds(per_chunk * h, per_chunk)
@@ -104,6 +104,10 @@
         loads.append(pltpu.make_async_copy(a, b, load_sem.at[1 + CHUNKS + k]))
     for copy in loads:
         copy.start()
+    barrier = pltpu.get_barrier_semaphore()
+    for axis in AXES:
+        tell(barrier, axis, low[axis])
+        tell(barrier, axis, high[axis])
 
     plan = wave_plan(sizes)
     wave_at = [0]
@@ -166,11 +170,7 @@
     loads[0].wait()
     lys[0:cx, :] = lab[pl.ds(0, cx, stride=cy), :]
     lys[cx : 2 * cx, :] = lab[pl.ds(cy - 1, cx, stride=cy), :]
-    for copy in loads[1:]:
-        copy.wait()
     pl.semaphore_wait(barrier, 2 * len(AXES))
-    wave_send()
-    first_x = [x_faces(field, xr_b, h) for h in range(CHUNKS)]
     label_copies = [
         ex.start(lab.at[0:8, :], lxr.at[1], "gx", low["gx"]),
         ex.start(lab.at[cells_xy - 8 : cells_xy, :], lxr.at[0], "gx", high["gx"]),
@@ -179,6 +179,11 @@
         ex.start(lab, lzr.at[1], "gz", low["gz"]),
         ex.start(lab, lzr.at[0], "gz", high["gz"]),
     ]
+    wave_send()
+    first_x = []
+    for h in range(CHUNKS):
+        loads[1 + h].wait()
+        first_x.append(x_faces(field, xr_b, h))
     first_y = []
     for h in range(CHUNKS):
         for s in range(per_chunk * h, per_chunk * (h + 1)):
@@ -197,6 +202,9 @@
     )
     first_z = z_faces(zs_b, zr_b)
 
+    for copy in loads[1 + CHUNKS :]:
+        copy.wait()
+
     wanted = send_map[...]
     key = lax.shift_right_arithmetic(wanted, 10) * lanes + (wanted & (lanes - 1))
     y_of = lax.shift_right_arithmetic(wanted, 7) & (cy - 1)
@@ -206,7 +214,8 @@
     rows_in = lax.broadcasted_iota(jnp.int32, (total_slots, slots.shape[1]), 0)
     slot_cap, slot_y = slots[...] % cap, slots[...] // cap % ny
     slot_row = slot_y * (nx * cap) + slot_cap * nx + slots[...] // (cap * ny)
-    pick[...] = jnp.where(rows_in == slot_row, 1.0, 0.0).astype(BF16)
+    pick_v[...] = jnp.where(rows_in == slot_row, 1.0, 0.0).astype(BF16)
+    pick_b[...] = jnp.where(rows_in == slots[...], 1.0, 0.0).astype(BF16)
     wave()
 
     for copy in label_copies:
@@ -367,7 +376,7 @@
         rows = source.shape[0] // count[axis]
         mine = pl.ds(pl.multiple_of(me[axis] * rows, rows), rows)
         copies = []
-        for d in range(1, count[axis]):
+        for d in farthest_first(count[axis]):
             partner = lax.rem(me[axis] + d, count[axis])
             theirs = pl.ds(pl.multiple_of(partner * rows, rows), rows)
             copies.append(ex.start(source.at[theirs, :], target.at[mine, :], axis, partner))
@@ -377,7 +386,7 @@
     def spread_slabs(source, target, axis):
         mine = me[axis]
         copies = []
-        for d in range(1, count[axis]):
+        for d in farthest_first(count[axis]):
             partner = lax.rem(mine + d, count[axis])
             copies.append(ex.start(source.at[partner], target.at[mine], axis, partner))
         target[mine] = source[mine]
@@ -446,8 +455,8 @@
             preferred_element_type=F32,
         )[0:1, :]
 
-    def select(fin):
-        columns = unpack(fin).T
+    def select(rows, pick):
+        columns = rows.T
         coarse = columns.astype(BF16)
         fine = (columns - coarse.astype(F32)).astype(BF16)
         return jnp.dot(coarse, pick[...], preferred_element_type=F32) + jnp.dot(
@@ -474,36 +483,39 @@
     slopes_of(field, xr_b, yr_b, image)
     early = lane_sums(moment_rows(0) + moment_rows(1) + moment_rows(2) + blank * (sensors // 8))
     gather(line_b)
-    line_b_copies = spread(line_b, mid_b, "gx")
+    regroup(line_b, out_b)
+    wave(len(plan))
+    out_b_copies = spread_slabs(out_b, fin_b, "gy")
     wait(second_z)
     merge_z(zr_v)
     for h in range(CHUNKS):
         wait(second[h])
         lax.fori_loop(steps_per_chunk * h, steps_per_chunk * (h + 1), energy_pass, 0)
     partial = early + lane_sums(blank * (3 * sensors // 8) + moment_rows(3))
-    wave(len(plan))
     plane = [
         {"gx": lax.rem(me["gx"] + dx, nx), "gz": lax.rem(me["gz"] + dz, nz)}
-        for dx in range(nx)
-        for dz in range(nz)
+        for dx in farthest_first(nx) + [0]
+        for dz in farthest_first(nz) + [0]
         if dx or dz
     ]
     plane_copies = reduce_start(red_plane, partial, plane)
-    wait(line_b_copies)
-    regroup(mid_b, out_b)
-    out_b_copies = spread_slabs(out_b, fin_b, "gy")
     slopes_of(image, xr_v, yr_v, None)
     gather(line_v)
     line_v_copies = spread(line_v, mid_v, "gx")
-    line = [{"gy": lax.rem(me["gy"] + d, ny)} for d in range(1, ny)]
+    line = [{"gy": lax.rem(me["gy"] + d, ny)} for d in farthest_first(ny)]
     line_copies = reduce_start(red_line, reduce_end(red_plane, plane_copies), line)
     wait(line_v_copies)
     regroup(mid_v, out_v)
     out_v_copies = spread_slabs(out_v, fin_v, "gy")
     wait(out_b_copies)
-    owned_b_out[...] = select(fin_b)
+    mid_b[...] = unpack(fin_b)
+    for ix in range(nx):
+        turn_b[ix * ny * cap : (ix + 1) * ny * cap, :] = mid_b[pl.ds(ix, ny * cap, stride=nx), :]
+    last_b_copies = spread(turn_b, last_b, "gx")
+    wait(last_b_copies)
+    owned_b_out[...] = select(last_b[...], pick_b)
     wait(out_v_copies)
-    owned_v_out[...] = select(fin_v)
+    owned_v_out[...] = select(unpack(fin_v), pick_v)
     moments_out[...] = jnp.broadcast_to(reduce_end(red_line, line_copies), (8, lanes))
 
 
@@ -575,10 +587,11 @@
         vmem((3, sensors * 8, cx * lanes), BF16),
         vmem((cx * lanes, total), BF16),
         vmem((total, owned), BF16),
+        vmem((total, owned), BF16),
         vmem((total // lanes, sensors * 8, lanes), F32),
     ]
     slabs = (sizes[1], total // sizes[1] * 3 // 4, lanes)
-    scratch += [vmem((total, lanes), F32)] * 4
+    scratch += [vmem((total, lanes), F32)] * 6
     scratch += [vmem(slabs, F32)] * 4
     scratch += [
         vmem((4, sensors * 8, lanes), F32),

time: 44.6 us -> 41 us (0.919)
  Pallas kernels: 43.7 us -> 39.8 us
    pallas_call x1, Pallas kernels: 42.5 us -> 38.6 us  [per_device(): pl.pallas_call(functools.partial(kernel, sizes), out_shape=(jax.ShapeDtyp...]
where the time goes in v4:
time: 41 us; the launch traced here: 40.4 us
  Pallas kernels  39.8 us (97%)
  between operations  0.66 us (2%)
    pallas_call x1, Pallas kernels, per_device(): pl.pallas_call(functools.partial(kernel, sizes), out_shape=(jax.ShapeDtyp...  38.6 us
    pallas_call x1, Pallas kernels, per_device(): pl.pallas_call(finish, out_shape=(jax.ShapeDtypeStruct((3, times, owned),...  1.17 us

profile of v4, /device:TPU:1, one launch (start us, length us, event | category | flops | bytes accessed | tf_op | source)
XLA Modules:
  0.0 40.4 jit_solution(17958645839671812330)
XLA Ops:
  0.6 0.0 copy-start
  0.6 38.6 %solve.1 = (f32[8,128]{1,0:T(8,128)S(1)}, f32[128,128]{1,0:T(8,128)S(1)}, f32[128,128]{1,0:T(8,128)S(1)}) custom-call(f32[32,32,128]{2,1,0:T(8,128)} %bitcast.4, s32[32,128]{1,0:T(8,128)} %bitcast.5, f32[6]{0:T(128)} %table_in.1, s32[1,256]{1,0:T(1,128)} %bitcast.6, s32[1,128]{1,0:T(1,128)} %bitcast.7), custom_call_target="tpu_custom_call" | custom-call | tf_op jit(solution)/shard_map/solve/pallas_call | solution.py:606
  39.2 0.0 copy-done
  39.3 1.2 %finish.1 = (f32[3,128,128]{2,1,0:T(8,128)}, f32[6,128]{1,0:T(8,128)}) custom-call(f32[8,128]{1,0:T(8,128)S(1)} %get-tuple-element.5.moments_in, f32[128,128]{1,0:T(8,128)S(1)} %get-tuple-element.6.owned_b, f32[128,128]{1,0:T(8,128)S(1)} %get-tuple-element.7.owned_v, f32[32,128]{1,0:T(8,128)S(1)} %copy-done), custom_call_target="tpu_custom_call" | custom-call | tf_op jit(solution)/shard_map/finish/pallas_call | solution.py:632
Async XLA Ops:
  0.6 38.6 %copy-start = (f32[32,128]{1,0:T(8,128)S(1)}, f32[32,128]{1,0:T(8,128)}, u32[]{:S(2)}) copy-start(f32[32,128]{1,0:T(8,128)} %data.1) | copy-start | bytes 49156

commit v5 on v4

--- a/solution.py
+++ b/solution.py
@@ -18,11 +18,8 @@
     def __init__(self, send, recv):
         self.send, self.recv, self.used = send, recv, 0
 
-    def start(self, source, target, axis, partner):
-        return self.start_at(source, target, {axis: partner})
-
-    def start_at(self, source, target, where):
-        copy = pltpu.make_async_remote_copy(
+    def copy(self, source, target, where):
+        return pltpu.make_async_remote_copy(
             src_ref=source,
             dst_ref=target,
             send_sem=self.send.at[self.used],
@@ -30,19 +27,20 @@
             device_id=where,
             device_id_type=pl.DeviceIdType.MESH,
         )
+
+    def start(self, copies, arrived):
+        for source, target, where in copies:
+            self.copy(source, target, where).start()
+        whole = self.copy(arrived, arrived, copies[0][2])
         self.used += 1
-        copy.start()
-        return copy
+        return whole
 
 
 CHUNKS = 2
 UNROLL = 8
 
 
-def copies_needed(sizes):
-    nx, ny, nz = sizes
-    plane = nx * nz - 1
-    return 6 + 2 * (4 * CHUNKS + 2) + plane + 3 * (ny - 1) + 2 * (nx - 1)
+GROUPS = 3 + 2 * (2 * CHUNKS + 1) + 4 + 2
 
 
 def farthest_first(size):
@@ -113,47 +111,51 @@
     wave_at = [0]
 
     def wave_sems(k, axis):
-        first = 2 * (len(AXES) * k + AXES.index(axis))
-        return wave_sem.at[first], wave_sem.at[first + 1]
+        return wave_sem.at[len(AXES) * k + AXES.index(axis)]
 
     def wave_send():
         k = wave_at[0]
         if k < len(plan):
             for axis, stride in plan[k]:
-                down, up = wave_sems(k, axis)
-                tell(down, axis, lax.rem(me[axis] + count[axis] - stride, count[axis]))
-                tell(up, axis, lax.rem(me[axis] + stride, count[axis]))
+                sem = wave_sems(k, axis)
+                tell(sem, axis, lax.rem(me[axis] + count[axis] - stride, count[axis]))
+                tell(sem, axis, lax.rem(me[axis] + stride, count[axis]))
 
     def wave(times=1):
         for _ in range(times):
             k = wave_at[0]
             if k < len(plan):
                 for axis, _stride in plan[k]:
-                    for sem in wave_sems(k, axis):
-                        pl.semaphore_wait(sem, 1)
+                    pl.semaphore_wait(wave_sems(k, axis), 2)
                 wave_at[0] += 1
                 wave_send()
+
+    def both_ways(to_low, to_high, target, arrived, axis):
+        copies = (
+            (to_low, target(1), {axis: low[axis]}),
+            (to_high, target(0), {axis: high[axis]}),
+        )
+        return [ex.start(copies, arrived)]
 
     def x_faces(whole, xr, h):
         part = pl.ds(per_chunk * h, per_chunk)
         last = cells_xy - 8
-        return [
-            ex.start(whole.at[part, 0:8, :], xr.at[1, part], "gx", low["gx"]),
-            ex.start(whole.at[part, last : last + 8, :], xr.at[0, part], "gx", high["gx"]),
-        ]
+        return both_ways(
+            whole.at[part, 0:8, :],
+            whole.at[part, last : last + 8, :],
+            lambda side: xr.at[side, part],
+            xr.at[:, part],
+            "gx",
+        )
 
     def y_faces(ys, yr, h):
         part = pl.ds(per_chunk * h * cx, per_chunk * cx)
-        return [
-            ex.start(ys.at[0, part], yr.at[1, part], "gy", low["gy"]),
-            ex.start(ys.at[1, part], yr.at[0, part], "gy", high["gy"]),
-        ]
+        return both_ways(
+            ys.at[0, part], ys.at[1, part], lambda side: yr.at[side, part], yr.at[:, part], "gy"
+        )
 
     def z_faces(zs, zr):
-        return [
-            ex.start(zs, zr.at[1], "gz", low["gz"]),
-            ex.start(zs, zr.at[0], "gz", high["gz"]),
-        ]
+        return both_ways(zs, zs, lambda side: zr.at[side], zr, "gz")
 
     def pack_z(values, s, acc):
         here = lax.shift_right_logical(lane, 1) == s
@@ -171,14 +173,11 @@
     lys[0:cx, :] = lab[pl.ds(0, cx, stride=cy), :]
     lys[cx : 2 * cx, :] = lab[pl.ds(cy - 1, cx, stride=cy), :]
     pl.semaphore_wait(barrier, 2 * len(AXES))
-    label_copies = [
-        ex.start(lab.at[0:8, :], lxr.at[1], "gx", low["gx"]),
-        ex.start(lab.at[cells_xy - 8 : cells_xy, :], lxr.at[0], "gx", high["gx"]),
-        ex.start(lys, lyr.at[1], "gy", low["gy"]),
-        ex.start(lys, lyr.at[0], "gy", high["gy"]),
-        ex.start(lab, lzr.at[1], "gz", low["gz"]),
-        ex.start(lab, lzr.at[0], "gz", high["gz"]),
-    ]
+    label_copies = (
+        both_ways(lab.at[0:8, :], lab.at[cells_xy - 8 : cells_xy, :], lambda side: lxr.at[side], lxr, "gx")
+        + both_ways(lys, lys, lambda side: lyr.at[side], lyr, "gy")
+        + both_ways(lab, lab, lambda side: lzr.at[side], lzr, "gz")
+    )
     wave_send()
     first_x = []
     for h in range(CHUNKS):
@@ -308,16 +307,6 @@
             acc = pack_z(results, s, acc)
         return acc
 
-    def energy_pass(i, carry):
-        for k in range(UNROLL):
-            s = UNROLL * i + k
-            own, near = neighbours(image, xr_v, yr_v, s, False)
-            term = own[0] * apply(own, near, 0)
-            for x in range(1, cx):
-                term = term + own[x] * apply(own, near, x)
-            mq[3, rows_of(s), :] = term
-        return carry
-
     def slope_pass(whole, xr, yr, result, i):
         slopes = [[[None, None] for _ in range(cx)] for _ in range(3)]
         for k in range(2):
@@ -332,9 +321,14 @@
                     q = result[s, 8 * x : 8 * x + 8, :]
                     for n, term in enumerate((own[x] * own[x], own[x] * q, q * q)):
                         sums[n] = term if sums[n] is None else sums[n] + term
+                else:
+                    term = own[x] * apply(own, near, x)
+                    sums[0] = term if sums[0] is None else sums[0] + term
             if result is not None:
                 for n in range(3):
                     mq[n, rows_of(s), :] = sums[n]
+            else:
+                mq[3, rows_of(s), :] = sums[0]
         at = pl.ds(pl.multiple_of(16 * i, 16), 16)
         for c in range(3):
             for x in range(cx):
@@ -343,13 +337,13 @@
                 ghi[c, at, x * lanes : (x + 1) * lanes] = coarse
                 glo[c, at, x * lanes : (x + 1) * lanes] = (slope - coarse.astype(F32)).astype(BF16)
 
-    def slopes_of(whole, xr, yr, result):
+    def slopes_of(whole, xr, yr, result, first=0, last=sensors):
         def step(i, carry):
             for k in range(UNROLL // 2):
                 slope_pass(whole, xr, yr, result, UNROLL // 2 * i + k)
             return carry
 
-        lax.fori_loop(0, sensors // UNROLL, step, 0)
+        lax.fori_loop(first // UNROLL, last // UNROLL, step, 0)
 
     def gather(line):
         parts = []
@@ -379,18 +373,20 @@
         for d in farthest_first(count[axis]):
             partner = lax.rem(me[axis] + d, count[axis])
             theirs = pl.ds(pl.multiple_of(partner * rows, rows), rows)
-            copies.append(ex.start(source.at[theirs, :], target.at[mine, :], axis, partner))
+            copies.append((source.at[theirs, :], target.at[mine, :], {axis: partner}))
+        arrived = ex.start(copies, target.at[pl.ds(0, rows * (count[axis] - 1)), :])
         target[mine, :] = source[mine, :]
-        return copies
+        return [arrived]
 
     def spread_slabs(source, target, axis):
         mine = me[axis]
         copies = []
         for d in farthest_first(count[axis]):
             partner = lax.rem(mine + d, count[axis])
-            copies.append(ex.start(source.at[partner], target.at[mine], axis, partner))
+            copies.append((source.at[partner], target.at[mine], {axis: partner}))
+        arrived = ex.start(copies, target.at[pl.ds(0, count[axis] - 1)])
         target[mine] = source[mine]
-        return copies
+        return [arrived]
 
     tail = lane >= 3 * sensors
     first_rows = row < 4
@@ -424,15 +420,13 @@
 
     def reduce_start(buffer, value, partners):
         buffer[0] = value
-        return [
-            ex.start_at(buffer.at[0], buffer.at[k + 1], where) for k, where in enumerate(partners)
-        ]
-
-    def reduce_end(buffer, copies):
-        for copy in copies:
-            copy.wait()
+        copies = [(buffer.at[0], buffer.at[k + 1], where) for k, where in enumerate(partners)]
+        return ex.start(copies, buffer.at[pl.ds(1, len(partners))])
+
+    def reduce_end(buffer, arrived):
+        arrived.wait()
         value = buffer[0]
-        for d in range(1, len(copies) + 1):
+        for d in range(1, buffer.shape[0]):
             value = value + buffer[d]
         return value
 
@@ -490,7 +484,7 @@
     merge_z(zr_v)
     for h in range(CHUNKS):
         wait(second[h])
-        lax.fori_loop(steps_per_chunk * h, steps_per_chunk * (h + 1), energy_pass, 0)
+        slopes_of(image, xr_v, yr_v, None, per_chunk * h, per_chunk * (h + 1))
     partial = early + lane_sums(blank * (3 * sensors // 8) + moment_rows(3))
     plane = [
         {"gx": lax.rem(me["gx"] + dx, nx), "gz": lax.rem(me["gz"] + dz, nz)}
@@ -499,7 +493,6 @@
         if dx or dz
     ]
     plane_copies = reduce_start(red_plane, partial, plane)
-    slopes_of(image, xr_v, yr_v, None)
     gather(line_v)
     line_v_copies = spread(line_v, mid_v, "gx")
     line = [{"gy": lax.rem(me["gy"] + d, ny)} for d in farthest_first(ny)]
@@ -558,7 +551,6 @@
     total = send_map.shape[-1]
     owned = owner_slots.shape[0]
     times = sensor_data.shape[1]
-    n = copies_needed(sizes)
     vmem = pltpu.VMEM
     scratch = [
         vmem((cells_xy, lanes), jnp.int32),
@@ -598,9 +590,9 @@
         vmem((sizes[0] * sizes[2], 1, lanes), F32),
         vmem((sizes[1], 1, lanes), F32),
         pltpu.SemaphoreType.DMA((4 + CHUNKS,)),
-        pltpu.SemaphoreType.DMA((n,)),
-        pltpu.SemaphoreType.DMA((n,)),
-        pltpu.SemaphoreType.REGULAR((2 * len(AXES) * len(wave_plan(sizes)),)),
+        pltpu.SemaphoreType.DMA((GROUPS,)),
+        pltpu.SemaphoreType.DMA((GROUPS,)),
+        pltpu.SemaphoreType.REGULAR((len(AXES) * len(wave_plan(sizes)),)),
     ]
     whole = pl.BlockSpec(memory_space=pltpu.VMEM)
     moments, owned_b, owned_v = pl.pallas_call(

time: 41 us -> 38.8 us (0.946)
  the two profiles are of different devices: /device:TPU:1 before, /device:TPU:32 now
where the time goes in v5:
time: 38.8 us; the launch traced here: 38.6 us
  Pallas kernels  37.9 us (98%)
  between operations  0.66 us (2%)
    pallas_call x1, Pallas kernels, per_device(): pl.pallas_call(functools.partial(kernel, sizes), out_shape=(jax.ShapeDtyp...  36.7 us
    pallas_call x1, Pallas kernels, per_device(): pl.pallas_call(finish, out_shape=(jax.ShapeDtypeStruct((3, times, owned),...  1.17 us

profile of v5, /device:TPU:32, one launch (start us, length us, event | category | flops | bytes accessed | tf_op | source)
XLA Modules:
  0.0 38.6 jit_solution(15340848577647478049)
XLA Ops:
  0.6 0.0 copy-start
  0.6 36.7 %solve.1 = (f32[8,128]{1,0:T(8,128)S(1)}, f32[128,128]{1,0:T(8,128)S(1)}, f32[128,128]{1,0:T(8,128)S(1)}) custom-call(f32[32,32,128]{2,1,0:T(8,128)} %bitcast.4, s32[32,128]{1,0:T(8,128)} %bitcast.5, f32[6]{0:T(128)} %table_in.1, s32[1,256]{1,0:T(1,128)} %bitcast.6, s32[1,128]{1,0:T(1,128)} %bitcast.7), custom_call_target="tpu_custom_call" | custom-call | tf_op jit(solution)/shard_map/solve/pallas_call | solution.py:598
  37.4 0.0 copy-done
  37.4 1.2 %finish.1 = (f32[3,128,128]{2,1,0:T(8,128)}, f32[6,128]{1,0:T(8,128)}) custom-call(f32[8,128]{1,0:T(8,128)S(1)} %get-tuple-element.5.moments_in, f32[128,128]{1,0:T(8,128)S(1)} %get-tuple-element.6.owned_b, f32[128,128]{1,0:T(8,128)S(1)} %get-tuple-element.7.owned_v, f32[32,128]{1,0:T(8,128)S(1)} %copy-done), custom_call_target="tpu_custom_call" | custom-call | tf_op jit(solution)/shard_map/finish/pallas_call | solution.py:624
Async XLA Ops:
  0.6 36.8 %copy-start = (f32[32,128]{1,0:T(8,128)S(1)}, f32[32,128]{1,0:T(8,128)}, u32[]{:S(2)}) copy-start(f32[32,128]{1,0:T(8,128)} %data.1) | copy-start | bytes 49156

commit v6 on v5

--- a/solution.py
+++ b/solution.py
@@ -37,7 +37,7 @@
 
 
 CHUNKS = 2
-UNROLL = 8
+UNROLL = 16
 
 
 GROUPS = 3 + 2 * (2 * CHUNKS + 1) + 4 + 2
@@ -111,7 +111,8 @@
     wave_at = [0]
 
     def wave_sems(k, axis):
-        return wave_sem.at[len(AXES) * k + AXES.index(axis)]
+        before = sum(len(steps) for steps in plan[:k])
+        return wave_sem.at[before + [step[0] for step in plan[k]].index(axis)]
 
     def wave_send():
         k = wave_at[0]
@@ -196,7 +197,7 @@
             sensors,
             lambda s, acc: pack_z([field[s, 8 * x : 8 * x + 8, :] for x in range(cx)], s, acc),
             no_z,
-            unroll=16,
+            unroll=32,
         ),
     )
     first_z = z_faces(zs_b, zr_b)
@@ -592,7 +593,7 @@
         pltpu.SemaphoreType.DMA((4 + CHUNKS,)),
         pltpu.SemaphoreType.DMA((GROUPS,)),
         pltpu.SemaphoreType.DMA((GROUPS,)),
-        pltpu.SemaphoreType.REGULAR((len(AXES) * len(wave_plan(sizes)),)),
+        pltpu.SemaphoreType.REGULAR((sum(len(steps) for steps in wave_plan(sizes)),)),
     ]
     whole = pl.BlockSpec(memory_space=pltpu.VMEM)
     moments, owned_b, owned_v = pl.pallas_call(

time: 38.8 us -> 39.1 us (level)
  the two profiles are of different devices: /device:TPU:32 before, /device:TPU:1 now
where the time goes in v6:
time: 39.1 us; the launch traced here: 38.5 us
  Pallas kernels  37.8 us (97%)
  between operations  0.66 us (2%)
    pallas_call x1, Pallas kernels, per_device(): pl.pallas_call(functools.partial(kernel, sizes), out_shape=(jax.ShapeDtyp...  36.6 us
    pallas_call x1, Pallas kernels, per_device(): pl.pallas_call(finish, out_shape=(jax.ShapeDtypeStruct((3, times, owned),...  1.17 us

profile of v6, /device:TPU:1, one launch (start us, length us, event | category | flops | bytes accessed | tf_op | source)
XLA Modules:
  0.0 38.5 jit_solution(10393533171396025660)
XLA Ops:
  0.6 0.0 copy-start
  0.6 36.6 %solve.1 = (f32[8,128]{1,0:T(8,128)S(1)}, f32[128,128]{1,0:T(8,128)S(1)}, f32[128,128]{1,0:T(8,128)S(1)}) custom-call(f32[32,32,128]{2,1,0:T(8,128)} %bitcast.4, s32[32,128]{1,0:T(8,128)} %bitcast.5, f32[6]{0:T(128)} %table_in.1, s32[1,256]{1,0:T(1,128)} %bitcast.6, s32[1,128]{1,0:T(1,128)} %bitcast.7), custom_call_target="tpu_custom_call" | custom-call | tf_op jit(solution)/shard_map/solve/pallas_call | solution.py:599
  37.3 0.0 copy-done
  37.3 1.2 %finish.1 = (f32[3,128,128]{2,1,0:T(8,128)}, f32[6,128]{1,0:T(8,128)}) custom-call(f32[8,128]{1,0:T(8,128)S(1)} %get-tuple-element.5.moments_in, f32[128,128]{1,0:T(8,128)S(1)} %get-tuple-element.6.owned_b, f32[128,128]{1,0:T(8,128)S(1)} %get-tuple-element.7.owned_v, f32[32,128]{1,0:T(8,128)S(1)} %copy-done), custom_call_target="tpu_custom_call" | custom-call | tf_op jit(solution)/shard_map/finish/pallas_call | solution.py:625
Async XLA Ops:
  0.6 36.7 %copy-start = (f32[32,128]{1,0:T(8,128)S(1)}, f32[32,128]{1,0:T(8,128)}, u32[]{:S(2)}) copy-start(f32[32,128]{1,0:T(8,128)} %data.1) | copy-start | bytes 49156
